TPU v7x, 32 devices: a whole 2x2x4 slice. The times are simulated.
32 devices in a mesh: groups: 2 (over y), cand: 4 (over z), mp: 4 (over x, core).
Axes of the slice: x: 2, y: 2, z: 4, core: 2. Of those that a mesh axis runs over, the one named last changes fastest.
Arguments:
- user_feats: bfloat16 [8, 4096], P(('groups', 'cand')), parts along dimension 0, may hold values from -6 to 6
- user_slot: int32 [2], P('groups'), parts along dimension 0, may hold values from 0 to 3, as said below
- cand_pool: bfloat16 [512, 4096], P('groups'), parts along dimension 0, may hold values from -6 to 6
- cand_ids: int32 [2, 64], P('groups'), parts along dimension 0, may hold values from 0 to 255
- first_weight: bfloat16 [8192, 8192], P('mp', 'cand'), may hold values from -0.0625 to 0.0625
- first_bias: float32 [8192], P('cand'), may hold values from -5 to 5
- second_weight: bfloat16 [8192, 8192], P('cand', 'mp'), may hold values from -0.0625 to 0.0625
- second_bias: float32 [8192], P('mp'), may hold values from -5 to 5
- third_weight: bfloat16 [8192, 8192], P('mp', 'cand'), may hold values from -0.0625 to 0.0625
- third_bias: float32 [8192], P('cand'), may hold values from -5 to 5
- score_weight: bfloat16 [8192], P('cand'), may hold values from -0.0625 to 0.0625
Outputs:
- crossed: bfloat16 [128, 8192], P(('groups', 'mp'), 'cand'), parts along dimension 0
- logits: float32 [128], P(('groups', 'mp')), parts along dimension 0
There are 2 independent parts, one for each index of `groups`. A program takes and returns all parts, laid end to end along the dimension named above; an argument that names none is the same for every part. Nothing has to cross between parts.
Inputs may be any that keep to these rules, and one draw needn't show every extreme that they name: `user_slot`: the users' slots are distinct.
All inputs are finite; a program needn't handle non-finite values.
Results may differ from a plain program's by a relative error of at most 0.022.
Values may be sent and summed in bfloat16 or wider, within the bound.
A program may use at most 64 MiB of HBM per device.

v0:
```python
import jax
import jax.numpy as jnp
from jax import lax
from jax.experimental import pallas as pl
from jax.experimental.pallas import tpu as pltpu
from jax.sharding import PartitionSpec as P

MESH = pl.DeviceIdType.MESH
F32 = jnp.float32
BF16 = jnp.bfloat16


def reverse_bits(value, bits):
    out = 0
    for _ in range(bits):
        out = 2 * out + value % 2
        value //= 2
    return out


def hand_on(crossed_ref, logit_ref, crossed_hbm, logit_hbm, sem):
    copies = [
        pltpu.make_async_copy(crossed_ref, crossed_hbm, sem.at[0]),
        pltpu.make_async_copy(logit_ref, logit_hbm, sem.at[1]),
    ]
    for copy in copies:
        copy.start()
    for copy in copies:
        copy.wait()


def make_kernel(n_mp, n_cand, shapes):
    rows, per_user, users, slots_each, half_width, pool_count, feat, col, n1, n2 = shapes
    cw1, cw2 = col // n1, feat // n2
    bits = n_mp.bit_length() - 1
    block = rows // n_mp
    ratio = feat // col
    group = n_mp * n_cand

    def kernel(
        user_hbm, slot_ref, pool_hbm, ids_hbm, w1_hbm, b1_hbm, w2_hbm, b2_hbm, w3_hbm, b3_hbm, score_hbm,
        out_ref, logit_ref,
        user_ref, ids_ref, b1_ref, b2_ref, b3_ref, score_ref, small_sem, slots, pool_v, w1_v, w2_v, w3_v, onehot, base_mp, base_col,
        acc1, send1, recv1, cross1, acc2, q_send, l_recv, r_recv, l_send, r_send, x3, acc3, send3, recv3, q_rows, q_all,
        w_sem, user_ss, user_rs, a_ss, a_rs, g_ss, g_rs, l_ss, l_rs, r_ss, r_rs, c_ss, c_rs, q_ss, q_rs,
    ):
        i = lax.axis_index("mp")
        j = lax.axis_index("cand")
        me = i * n_cand + j
        pending = []

        def remote(src, dst, ss, rs, where):
            return pltpu.make_async_remote_copy(
                src_ref=src, dst_ref=dst, send_sem=ss, recv_sem=rs, device_id=where, device_id_type=MESH
            )

        small_copies = [
            pltpu.make_async_copy(src, dst, small_sem.at[k])
            for k, (src, dst) in enumerate(
                (
                    (user_hbm, user_ref), (ids_hbm, ids_ref), (b1_hbm, b1_ref),
                    (b2_hbm, b2_ref), (b3_hbm, b3_ref), (score_hbm, score_ref),
                )
            )
        ]
        for copy in small_copies:
            copy.start()
        barrier = pltpu.get_barrier_semaphore()

        def greet(d, carry):
            peer = lax.rem(me + d, group)
            pl.semaphore_signal(
                barrier, inc=1, device_id={"mp": peer // n_cand, "cand": lax.rem(peer, n_cand)}, device_id_type=MESH
            )
            return carry

        lax.fori_loop(1, group, greet, 0)

        pool_copy = pltpu.make_async_copy(pool_hbm, pool_v, w_sem.at[0])
        w1_copies = [
            pltpu.make_async_copy(w1_hbm.at[:, pl.ds(c * cw1, cw1)], w1_v.at[c], w_sem.at[1 + c]) for c in range(n1)
        ]
        w2_copies = [
            pltpu.make_async_copy(w2_hbm.at[pl.ds(c * cw1, cw1), :], w2_v.at[pl.ds(c * cw1, cw1), :], w_sem.at[1 + n1 + c])
            for c in range(n1)
        ]
        w3_copies = [
            pltpu.make_async_copy(w3_hbm.at[pl.ds(c * cw2, cw2), :], w3_v.at[pl.ds(c * cw2, cw2), :], w_sem.at[1 + 2 * n1 + c])
            for c in range(n2)
        ]
        pool_copy.start()
        for copy in w1_copies:
            copy.start()

        small_copies[0].wait()
        pl.semaphore_wait(barrier, group - 1)

        def user_copy(d):
            return remote(
                user_ref, slots.at[j], user_ss.at[d - 1], user_rs.at[j], {"cand": lax.rem(j + d, n_cand)}
            )

        for d in range(1, n_cand):
            user_copy(d).start()
        slots[j] = user_ref[...]
        small_copies[1].wait()

        for u in range(users):
            hot = (
                lax.broadcasted_iota(jnp.int32, (pool_count, per_user), 0) == ids_ref[u : u + 1, :]
            ).astype(F32).T
            for p in range(n_mp):
                first = reverse_bits(p, bits) * block
                if first // per_user == u:
                    off = first % per_user
                    onehot[p * block : (p + 1) * block, :] = hot[off : off + block].astype(BF16)

        def from_pool(dst, index, width):
            @pl.when(index >= half_width // width)
            def _():
                for c in range(0, width, 256):
                    start = pl.multiple_of(index * width - half_width + c, 128)
                    dst[:, c : c + 256] = jnp.dot(
                        onehot[...], pool_v[:, pl.ds(start, 256)], preferred_element_type=F32
                    ).astype(BF16)

        def from_user(dst, index, width):
            @pl.when(index < half_width // width)
            def _():
                start = pl.multiple_of(index * width, 128)
                for p in range(n_mp):
                    slot = slot_ref[(reverse_bits(p, bits) * block) // per_user]
                    row = slots[slot // slots_each, :, pl.ds(start, width)].astype(F32)
                    if slots_each > 1:
                        pick = lax.broadcasted_iota(jnp.int32, row.shape, 0) == lax.rem(slot, slots_each)
                        row = jnp.sum(jnp.where(pick, row, 0.0), axis=0, keepdims=True)
                    dst[p * block : (p + 1) * block, :] = jnp.broadcast_to(row, (block, width)).astype(BF16)

        def from_all_users():
            for d in range(1, n_cand):
                k = lax.rem(j - d + n_cand, n_cand)
                remote(user_ref, slots.at[k], user_ss.at[d - 1], user_rs.at[k], {"cand": k}).wait_recv()

        pool_copy.wait()
        from_pool(base_mp, i, feat)
        user_side = i < half_width // feat

        @pl.when(user_side)
        def _():
            from_pool(base_col, j, col)
            from_all_users()
            from_user(base_mp, i, feat)

        def bit_of(b):
            return lax.rem(i // (1 << b), 2)

        def partner(b):
            return i + (1 << b) * (1 - 2 * bit_of(b))

        lows = [0]
        for b in range(bits):
            lows.append(lows[b] + bit_of(b) * (rows >> (b + 1)))

        def seg(b):
            size = rows >> b
            if b == 0:
                return pl.ds(0, rows)
            return pl.ds(pl.multiple_of(lows[b], size), size)

        def other(b):
            size = rows >> (b + 1)
            low = lows[b] + (1 - bit_of(b)) * size
            return pl.ds(pl.multiple_of(low, size), size)

        last = bits - 1

        def scatter_copy(c, b):
            rng = other(b) if b < last else seg(b)
            size = rows >> min(b + 1, last)
            return remote(
                send1.at[c, rng, :], recv1.at[b, c, pl.ds(0, size), :], a_ss.at[b, c], a_rs.at[b, c], {"mp": partner(b)}
            )

        def gather_copy(c, b):
            return remote(
                cross1.at[c, seg(b + 1), :], cross1.at[c, seg(b + 1), :], g_ss.at[b, c], g_rs.at[b, c], {"mp": partner(b)}
            )

        def gather_wait(c, b):
            remote(
                cross1.at[c, other(b), :], cross1.at[c, other(b), :], g_ss.at[b, c], g_rs.at[b, c], {"mp": partner(b)}
            ).wait_recv()

        def stage_a(c):
            w1_copies[c].wait()
            term = jnp.dot(base_mp[...], w1_v[c], preferred_element_type=F32)
            acc1[c] = term
            send1[c] = term.astype(BF16)
            copy = scatter_copy(c, 0)
            copy.start()
            pending.append(copy)

        def stage_b(c):
            for b in range(last):
                scatter_copy(c, b).wait_recv()
                size = rows >> (b + 1)
                term = acc1[c, seg(b + 1), :] + recv1[b, c, 0:size, :].astype(F32)
                if b + 1 < last:
                    acc1[c, seg(b + 1), :] = term
                send1[c, seg(b + 1), :] = term.astype(BF16)
                copy = scatter_copy(c, b + 1)
                copy.start()
                pending.append(copy)

        def stage_c(c):
            scatter_copy(c, last).wait_recv()
            size = rows >> last
            total = send1[c, seg(last), :].astype(F32) + recv1[last, c, 0:size, :].astype(F32)
            cols = slice(c * cw1, (c + 1) * cw1)
            base = base_col[seg(last), cols].astype(F32)
            cross1[c, seg(last), :] = (base * (total + b1_ref[:, cols]) + base).astype(BF16)
            if last > 0:
                copy = gather_copy(c, last - 1)
                copy.start()
                pending.append(copy)

        def line_copy(n, right, first):
            src = (q_send if first else (l_send if right else r_send)).at[n]
            if right:
                return remote(src, l_recv.at[n], l_ss.at[n], l_rs.at[n], {"cand": j + 1})
            return remote(src, r_recv.at[n], r_ss.at[n], r_rs.at[n], {"cand": j - 1})

        def stage_d(c):
            for b in range(last - 1, -1, -1):
                gather_wait(c, b)
                if b > 0:
                    copy = gather_copy(c, b - 1)
                    copy.start()
                    pending.append(copy)
            w2_copies[c].wait()
            for n in range(n2):
                cols = slice(n * cw2, (n + 1) * cw2)
                term = jnp.dot(
                    cross1[c], w2_v[c * cw1 : (c + 1) * cw1, cols], preferred_element_type=F32
                )
                if c > 0:
                    term = acc2[:, cols] + term
                if c < n1 - 1:
                    acc2[:, cols] = term
                    continue
                owner = (j == i * ratio + (n * cw2) // col).astype(F32)
                inner = (n * cw2) % col
                carried = cross1[inner // cw1, :, inner % cw1 : inner % cw1 + cw2].astype(F32)
                term = base_mp[:, cols].astype(F32) * (term + owner * b2_ref[:, cols]) + owner * carried
                q_send[n] = term.astype(BF16)

                @pl.when(j == 0)
                def _():
                    line_copy(n, True, True).start()

                @pl.when(j == n_cand - 1)
                def _():
                    line_copy(n, False, True).start()

        order = []
        for s in range(n1 + 1):
            if s < n1:
                order.append((stage_a, s))
            if s >= 1:
                order.append((stage_b, s - 1))
        for s in range(n1 + 1):
            if s < n1:
                order.append((stage_c, s))
            if s >= 1:
                order.append((stage_d, s - 1))
        started = False
        for stage, c in order:
            if stage is stage_c and c == 0:
                @pl.when(jnp.logical_not(user_side))
                def _():
                    from_pool(base_col, j, col)
                    from_all_users()

                from_user(base_col, j, col)
                for copy in small_copies[2:]:
                    copy.wait()
            stage(c)
            if stage is stage_a and c == n1 - 1:
                for copy in w2_copies:
                    copy.start()
            if stage is stage_c and not started:
                started = True
                for copy in w3_copies:
                    copy.start()

        def forward(n, right):
            came = (l_recv if right else r_recv)[n].astype(F32)
            (l_send if right else r_send)[n] = (came + q_send[n].astype(F32)).astype(BF16)
            line_copy(n, right, False).start()

        def take(n, right):
            if right:
                remote(l_send.at[n], l_recv.at[n], l_ss.at[n], l_rs.at[n], {"cand": j}).wait_recv()
            else:
                remote(r_send.at[n], r_recv.at[n], r_ss.at[n], r_rs.at[n], {"cand": j}).wait_recv()

        def third(n):
            w3_copies[n].wait()
            for p in range(n1):
                cols = slice(p * cw1, (p + 1) * cw1)
                term = jnp.dot(
                    x3[:, n * cw2 : (n + 1) * cw2], w3_v[n * cw2 : (n + 1) * cw2, cols], preferred_element_type=F32
                )
                if n > 0:
                    term = acc3[:, cols] + term
                acc3[:, cols] = term

        skew = min(4, n2)
        near_left = j < (n_cand + 1) // 2
        inner_device = jnp.logical_and(j > 0, j < n_cand - 1)
        for s in range(n2 + skew):
            if s < n2:
                @pl.when(jnp.logical_and(inner_device, near_left))
                def _():
                    take(s, True)
                    forward(s, True)

                @pl.when(jnp.logical_and(inner_device, jnp.logical_not(near_left)))
                def _():
                    take(s, False)
                    forward(s, False)

            n = s - skew
            if n < 0:
                continue

            @pl.when(jnp.logical_and(inner_device, near_left))
            def _():
                take(n, False)
                forward(n, False)

            @pl.when(jnp.logical_and(inner_device, jnp.logical_not(near_left)))
            def _():
                take(n, True)
                forward(n, True)

            cols = slice(n * cw2, (n + 1) * cw2)

            @pl.when(inner_device)
            def _():
                x3[:, cols] = (
                    q_send[n].astype(F32) + l_recv[n].astype(F32) + r_recv[n].astype(F32)
                ).astype(BF16)

            @pl.when(j == 0)
            def _():
                take(n, False)
                x3[:, cols] = (q_send[n].astype(F32) + r_recv[n].astype(F32)).astype(BF16)

            @pl.when(j == n_cand - 1)
            def _():
                take(n, True)
                x3[:, cols] = (q_send[n].astype(F32) + l_recv[n].astype(F32)).astype(BF16)

            third(n)

        def last_copy(c, b):
            size = rows >> (b + 1)
            return remote(
                send3.at[c, other(b), :], recv3.at[b, c, pl.ds(0, size), :], c_ss.at[b, c], c_rs.at[b, c], {"mp": partner(b)}
            )

        owner = (i == j // ratio).astype(F32)
        lanes = jnp.zeros((rows, 128), F32)
        for c in range(n1):
            cols = slice(c * cw1, (c + 1) * cw1)
            if ratio == 1:
                carried = x3[:, cols]
            else:
                carried = x3[:, pl.ds(pl.multiple_of(lax.rem(j, ratio) * col + c * cw1, 128), cw1)]
            term = (
                base_col[:, cols].astype(F32) * (acc3[:, cols] + owner * b3_ref[:, cols])
                + owner * carried.astype(F32)
            )
            acc3[:, cols] = term
            send3[c] = term.astype(BF16)
            copy = last_copy(c, 0)
            copy.start()
            pending.append(copy)
            scored = term * score_ref[cols].astype(F32).reshape(1, cw1)
            for k in range(0, cw1, 128):
                lanes = lanes + scored[:, k : k + 128]
        q_rows[...] = jnp.zeros_like(q_rows)
        q_rows[0:rows, :] = lanes
        q_all[me] = jnp.sum(q_rows[...].T, axis=0, keepdims=True)

        def q_copy(d):
            peer = lax.rem(me + d, group)
            return remote(
                q_all.at[me], q_all.at[me], q_ss.at[d], q_rs.at[me],
                {"mp": peer // n_cand, "cand": lax.rem(peer, n_cand)},
            )

        def q_start(d, carry):
            q_copy(d).start()
            return carry

        lax.fori_loop(1, group, q_start, 0)

        for b in range(bits):
            for c in range(n1):
                cols = slice(c * cw1, (c + 1) * cw1)
                last_copy(c, b).wait_recv()
                size = rows >> (b + 1)
                term = acc3[seg(b + 1), cols] + recv3[b, c, 0:size, :].astype(F32)
                if b + 1 < bits:
                    acc3[seg(b + 1), cols] = term
                    send3[c, seg(b + 1), :] = term.astype(BF16)
                    copy = last_copy(c, b + 1)
                    copy.start()
                    pending.append(copy)
                else:
                    out_ref[:, cols] = term.astype(BF16)

        def q_wait(d, carry):
            k = lax.rem(me - d + group, group)
            remote(q_all.at[k], q_all.at[k], q_ss.at[d], q_rs.at[k], {"cand": j}).wait_recv()
            return carry

        lax.fori_loop(1, group, q_wait, 0)
        total = jnp.sum(q_all[...], axis=0)
        for k in range(n_mp):
            p = reverse_bits(k, bits)

            @pl.when(i == k)
            def _():
                logit_ref[...] = total[:, p * block : (p + 1) * block]

        for copy in pending:
            copy.wait_send()
        for d in range(1, n_cand):
            user_copy(d).wait_send()

        def q_sent(d, carry):
            q_copy(d).wait_send()
            return carry

        lax.fori_loop(1, group, q_sent, 0)
        for n in range(n2):
            @pl.when(j < n_cand - 1)
            def _():
                line_copy(n, True, False).wait_send()

            @pl.when(j > 0)
            def _():
                line_copy(n, False, False).wait_send()

    return kernel


def solution(mesh):
    n_mp, n_cand = mesh.shape["mp"], mesh.shape["cand"]

    def body(
        user_feats, user_slot, cand_pool, cand_ids, first_weight, first_bias,
        second_weight, second_bias, third_weight, third_bias, score_weight,
    ):
        slots_each, half_width = user_feats.shape
        users, per_user = cand_ids.shape
        rows = users * per_user
        pool_count = cand_pool.shape[0]
        feat, col = first_weight.shape
        n1 = max(1, col // 512)
        n2 = max(1, feat // 256)
        cw1, cw2 = col // n1, feat // n2
        bits = n_mp.bit_length() - 1
        block = rows // n_mp
        group = n_mp * n_cand
        shapes = (rows, per_user, users, slots_each, half_width, pool_count, feat, col, n1, n2)
        vmem = pl.BlockSpec(memory_space=pltpu.VMEM)
        smem = pl.BlockSpec(memory_space=pltpu.SMEM)
        hbm = pl.BlockSpec(memory_space=pl.ANY)
        dma = pltpu.SemaphoreType.DMA
        exchange = rows >> (1 if bits > 1 else 0)
        crossed, logits = pl.pallas_call(
            make_kernel(n_mp, n_cand, shapes),
            out_shape=(
                pltpu.VMEM((block, col), BF16),
                pltpu.VMEM((1, block), F32),
            ),
            in_specs=[hbm, smem] + [hbm] * 9,
            out_specs=(vmem, vmem),
            scratch_shapes=[
                pltpu.VMEM((slots_each, half_width), BF16),
                pltpu.VMEM((users, per_user), jnp.int32),
                pltpu.VMEM((1, col), F32),
                pltpu.VMEM((1, feat), F32),
                pltpu.VMEM((1, col), F32),
                pltpu.VMEM((col,), BF16),
                dma((6,)),
                pltpu.VMEM((n_cand, slots_each, half_width), BF16),
                pltpu.VMEM((pool_count, half_width), BF16),
                pltpu.VMEM((n1, feat, cw1), BF16),
                pltpu.VMEM((col, feat), BF16),
                pltpu.VMEM((feat, col), BF16),
                pltpu.VMEM((rows, pool_count), BF16),
                pltpu.VMEM((rows, feat), BF16),
                pltpu.VMEM((rows, col), BF16),
                pltpu.VMEM((n1, rows, cw1), F32),
                pltpu.VMEM((n1, rows, cw1), BF16),
                pltpu.VMEM((bits, n1, exchange, cw1), BF16),
                pltpu.VMEM((n1, rows, cw1), BF16),
                pltpu.VMEM((rows, feat), F32),
                pltpu.VMEM((n2, rows, cw2), BF16),
                pltpu.VMEM((n2, rows, cw2), BF16),
                pltpu.VMEM((n2, rows, cw2), BF16),
                pltpu.VMEM((n2, rows, cw2), BF16),
                pltpu.VMEM((n2, rows, cw2), BF16),
                pltpu.VMEM((rows, feat), BF16),
                pltpu.VMEM((rows, col), F32),
                pltpu.VMEM((n1, rows, cw1), BF16),
                pltpu.VMEM((bits, n1, rows // 2, cw1), BF16),
                pltpu.VMEM((max(rows, 128), 128), F32),
                pltpu.VMEM((group, 1, max(rows, 128)), F32),
                dma((1 + 2 * n1 + n2,)),
                dma((n_cand,)),
                dma((n_cand,)),
                dma((bits, n1)),
                dma((bits, n1)),
                dma((bits, n1)),
                dma((bits, n1)),
                dma((n2,)),
                dma((n2,)),
                dma((n2,)),
                dma((n2,)),
                dma((bits, n1)),
                dma((bits, n1)),
                dma((group,)),
                dma((group,)),
            ],
            compiler_params=pltpu.CompilerParams(
                collective_id=0, has_side_effects=True, vmem_limit_bytes=67043328 - 3000 * 1024
            ),
        )(
            user_feats, user_slot, cand_pool, cand_ids, first_weight, first_bias.reshape(1, -1),
            second_weight, second_bias.reshape(1, -1), third_weight, third_bias.reshape(1, -1),
            score_weight,
        )
        crossed, logits = pl.pallas_call(
            hand_on,
            out_shape=(
                jax.ShapeDtypeStruct((block, col), BF16),
                jax.ShapeDtypeStruct((1, block), F32),
            ),
            in_specs=[vmem, vmem],
            out_specs=(hbm, hbm),
            scratch_shapes=[dma((2,))],
            compiler_params=pltpu.CompilerParams(vmem_limit_bytes=1024 * 1024),
        )(crossed, logits)
        return crossed, logits.reshape(-1)

    in_specs = (
        P(("groups", "cand"), None),
        P("groups"),
        P("groups", None),
        P("groups", None),
        P("mp", "cand"),
        P("cand"),
        P("cand", "mp"),
        P("mp"),
        P("mp", "cand"),
        P("cand"),
        P("cand"),
    )
    out_specs = (P(("groups", "mp"), "cand"), P(("groups", "mp")))
    return jax.shard_map(body, mesh=mesh, in_specs=in_specs, out_specs=out_specs, check_vma=False)
```

profile of v0, /device:TPU:0, one launch (start us, length us, event | category | flops | bytes accessed | tf_op | source)
XLA Modules:
  0.0 39.7 jit_solution(11286547125417754144)
XLA Ops:
  1.3 37.8 %shard_map.122 = (bf16[16,2048]{1,0:T(8,128)(2,1)S(1)}, f32[1,16]{1,0:T(1,128)S(1)}) custom-call(bf16[1,4096]{1,0:T(2,128)(2,1)} %user_hbm.1, s32[1]{0:T(128)S(6)} %copy.13.slot_ref, bf16[256,4096]{1,0:T(8,128)(2,1)} %pool_hbm.1, s32[1,64]{1,0:T(1,128)} %ids_hbm.1, bf16[2048,2048]{1,0:T(8,128)(2,1)} %w1_hbm.1, f32[1,2048]{1,0:T(1,128)} %bitcast.4, ...), custom_call_target="tpu_custom_call" | custom-call | tf_op jit(solution)/shard_map/pallas_call | solution.py:485
  39.0 0.7 %shard_map.123 = (bf16[16,2048]{1,0:T(8,128)(2,1)}, f32[1,16]{1,0:T(1,128)}) custom-call(bf16[16,2048]{1,0:T(8,128)(2,1)S(1)} %get-tuple-element.6.crossed_ref, f32[1,16]{1,0:T(1,128)S(1)} %get-tuple-element.7.logit_ref), custom_call_target="tpu_custom_call" | custom-call | tf_op jit(solution)/shard_map/pallas_call | solution.py:549
where the time goes:
time: 40 us; the launch traced here: 39.7 us
  Pallas kernels  38.4 us (96%)
  between operations  1.29 us (3%)
    pallas_call x1, Pallas kernels, body(): pl.pallas_call(make_kernel(n_mp, n_cand, shapes), out_shape=(pltpu.VMEM((...  37.8 us

commit v1 on v0

v1 whole, which is shorter than its diff:
```python
import contextlib

import jax
import jax.numpy as jnp
from jax import lax
from jax.experimental import pallas as pl
from jax.experimental.pallas import tpu as pltpu
from jax.sharding import PartitionSpec as P

MESH = pl.DeviceIdType.MESH
F32 = jnp.float32
BF16 = jnp.bfloat16


def scope(name):
    return contextlib.nullcontext()


def reverse_bits(value, bits):
    out = 0
    for _ in range(bits):
        out = 2 * out + value % 2
        value = value // 2
    return out


def hand_on(crossed_ref, logit_ref, crossed_hbm, logit_hbm, sem):
    copies = [
        pltpu.make_async_copy(crossed_ref, crossed_hbm, sem.at[0]),
        pltpu.make_async_copy(logit_ref, logit_hbm, sem.at[1]),
    ]
    for copy in copies:
        copy.start()
    for copy in copies:
        copy.wait()


def make_kernel(n_mp, n_cand, shapes):
    rows, per_user, users, slots_each, half_width, pool_count, feat, col, n1, n2, n3, lhs_rows = shapes
    cw1, cw2, cw3 = col // n1, feat // n2, col // n3
    bits = n_mp.bit_length() - 1
    low = bits - 1
    half = n_mp // 2
    block = rows // n_mp
    ratio = feat // col
    group = n_mp * n_cand
    part = rows // 2
    first_pool_col = half_width // col

    def user_of(p):
        return (reverse_bits(p, bits) * block) // per_user

    def kernel(
        user_hbm, slot_hbm, pool_hbm, ids_hbm, w1_hbm, b1_hbm, w2_hbm, b2_hbm, w3_hbm, b3_hbm, score_hbm,
        out_ref, logit_ref,
        slot_ref, user_ref, ids_ref, b1_ref, b2_ref, b3_ref, score_ref, small_sem, slots, pool_m, pool_c, w1_v, w2_v, w3_v,
        onehot, base_mp, base_col, lhs, acc1, send1, recv1, psum, ubuf, cross1, acc2, q_send, zr, zs, x3, acc3, send3, recv3,
        q_rows, q_all,
        w_sem, user_ss, user_rs, a_ss, a_rs, x_ss, x_rs, g_ss, g_rs, u_ss, u_rs, z_ss, z_rs, c_ss, c_rs, q_ss, q_rs,
    ):
        i = lax.axis_index("mp")
        j = lax.axis_index("cand")
        me = i * n_cand + j
        pending = []
        user_side = i < half
        pool_side = jnp.logical_not(user_side)

        def remote(src, dst, ss, rs, where):
            return pltpu.make_async_remote_copy(
                src_ref=src, dst_ref=dst, send_sem=ss, recv_sem=rs, device_id=where, device_id_type=MESH
            )

        barrier = pltpu.get_barrier_semaphore()
        with scope("greet"):
            def greet(d, carry):
                pl.semaphore_signal(barrier, inc=1, device_id={"cand": lax.rem(j + d, n_cand)}, device_id_type=MESH)
                return carry

            lax.fori_loop(1, n_cand, greet, 0, unroll=n_cand <= 4)
            for d in range(1, n_mp):
                pl.semaphore_signal(barrier, inc=1, device_id={"mp": lax.rem(i + d, n_mp)}, device_id_type=MESH)

        small_copies = [
            pltpu.make_async_copy(src, dst, small_sem.at[k])
            for k, (src, dst) in enumerate(
                (
                    (user_hbm, user_ref), (ids_hbm, ids_ref), (slot_hbm, slot_ref), (b1_hbm, b1_ref),
                    (b2_hbm, b2_ref), (b3_hbm, b3_ref), (score_hbm, score_ref),
                )
            )
        ]
        m_start = pl.multiple_of(jnp.maximum(i - half, 0) * feat, 128)
        c_start = pl.multiple_of(jnp.maximum(j - first_pool_col, 0) * col, 128)
        pool_m_copy = pltpu.make_async_copy(pool_hbm.at[:, pl.ds(m_start, feat)], pool_m, w_sem.at[0])
        pool_c_copy = pltpu.make_async_copy(pool_hbm.at[:, pl.ds(c_start, col)], pool_c, w_sem.at[1])
        w1_copies = [
            pltpu.make_async_copy(w1_hbm.at[:, pl.ds(c * cw1, cw1)], w1_v.at[c], w_sem.at[2 + c]) for c in range(n1)
        ]
        w2_copies = [
            pltpu.make_async_copy(w2_hbm.at[pl.ds(c * cw1, cw1), :], w2_v.at[pl.ds(c * cw1, cw1), :], w_sem.at[2 + n1 + c])
            for c in range(n1)
        ]
        w3_copies = [
            pltpu.make_async_copy(w3_hbm.at[pl.ds(c * cw2, cw2), :], w3_v.at[pl.ds(c * cw2, cw2), :], w_sem.at[2 + 2 * n1 + c])
            for c in range(n2)
        ]
        col_pool = j >= first_pool_col
        with scope("loads"):
            for copy in small_copies[:3]:
                copy.start()

            @pl.when(pool_side)
            def _():
                pool_m_copy.start()

            for copy in w1_copies:
                copy.start()
            for copy in small_copies[3:]:
                copy.start()

            @pl.when(col_pool)
            def _():
                pool_c_copy.start()

            end = jnp.logical_or(j == 0, j == n_cand - 1)
            inner = jnp.logical_not(end)
            nd = (j >= (n_cand + 1) // 2).astype(jnp.int32)

            @pl.when(end)
            def _():
                zr[nd] = jnp.zeros(zr.shape[1:], BF16)

        with scope("onehot"):
            small_copies[1].wait()
            for u in range(users):
                hot = (
                    lax.broadcasted_iota(jnp.int32, (pool_count, per_user), 0) == ids_ref[u : u + 1, :]
                ).astype(F32).T
                for p in range(n_mp):
                    first = reverse_bits(p, bits) * block
                    if first // per_user == u:
                        off = first % per_user
                        onehot[p * block : (p + 1) * block, :] = hot[off : off + block].astype(BF16)

        def from_pool(dst, src, width):
            for c in range(0, width, 256):
                dst[:, c : c + 256] = jnp.dot(onehot[...], src[:, c : c + 256], preferred_element_type=F32).astype(BF16)

        def user_row(u, index, width):
            start = pl.multiple_of(index * width, 128)
            slot = slot_ref[u]
            row = slots[slot // slots_each, :, pl.ds(start, width)].astype(F32)
            if slots_each > 1:
                pick = lax.broadcasted_iota(jnp.int32, row.shape, 0) == lax.rem(slot, slots_each)
                row = jnp.sum(jnp.where(pick, row, 0.0), axis=0, keepdims=True)
            return row

        def from_user(dst, index, width):
            rows_of = [user_row(u, index, width) for u in range(users)]
            for p in range(n_mp):
                dst[p * block : (p + 1) * block, :] = jnp.broadcast_to(rows_of[user_of(p)], (block, width)).astype(BF16)

        def user_copy(d):
            return remote(user_ref, slots.at[j], user_ss.at[d - 1], user_rs.at[j], {"cand": lax.rem(j + d, n_cand)})

        def from_all_users():
            for d in range(1, n_cand):
                k = lax.rem(j - d + n_cand, n_cand)
                remote(user_ref, slots.at[k], user_ss.at[d - 1], user_rs.at[k], {"cand": k}).wait_recv()
            small_copies[2].wait()

        def bit_of(b):
            return lax.rem(i // (1 << b), 2)

        def partner(b):
            return i + (1 << b) * (1 - 2 * bit_of(b))

        lows = [0]
        for b in range(bits):
            lows.append(lows[b] + bit_of(b) * (rows >> (b + 1)))

        def seg(b):
            size = rows >> b
            if b == 0:
                return pl.ds(0, rows)
            return pl.ds(pl.multiple_of(lows[b], size), size)

        def other(b):
            size = rows >> (b + 1)
            start = lows[b] + (1 - bit_of(b)) * size
            return pl.ds(pl.multiple_of(start, size), size)

        def scatter_copy(c, b):
            size = rows >> (b + 1)
            return remote(
                send1.at[c, other(b), :], recv1.at[b, c, pl.ds(0, size), :], a_ss.at[b, c], a_rs.at[b, c], {"mp": partner(b)}
            )

        def across_copy(c):
            return remote(
                psum.at[c, seg(low), :], psum.at[c, seg(low), :], x_ss.at[c], x_rs.at[c], {"mp": lax.rem(i + half, n_mp)}
            )

        def gather_copy(c, b):
            return remote(
                psum.at[c, seg(b + 1), :], psum.at[c, seg(b + 1), :], g_ss.at[b, c], g_rs.at[b, c], {"mp": partner(b)}
            )

        def gather_wait(c, b):
            remote(
                psum.at[c, other(b), :], psum.at[c, other(b), :], g_ss.at[b, c], g_rs.at[b, c], {"mp": partner(b)}
            ).wait_recv()

        def spread(c):
            if low > 0:
                gather_copy(c, low - 1).start()

        def stage_a(c):
            w1_copies[c].wait()
            term = jnp.dot(base_mp[...], w1_v[c], preferred_element_type=F32)
            if low > 0:
                acc1[c] = term
                send1[c] = term.astype(BF16)
            else:
                psum[c] = term.astype(BF16)

        def stage_b(c):
            for b in range(low):
                scatter_copy(c, b).wait_recv()
                size = rows >> (b + 1)
                term = acc1[c, seg(b + 1), :] + recv1[b, c, 0:size, :].astype(F32)
                if b + 1 < low:
                    acc1[c, seg(b + 1), :] = term
                    send1[c, seg(b + 1), :] = term.astype(BF16)
                    scatter_copy(c, b + 1).start()
                else:
                    psum[c, seg(low), :] = term.astype(BF16)
            across_copy(c).start()
            spread(c)

        def part_copy(c, d):
            return remote(ubuf.at[i, c], ubuf.at[i, c], u_ss.at[d, c], u_rs.at[i, c], {"mp": lax.rem(i + d, n_mp)})

        def part_wait(c, src):
            remote(ubuf.at[src, c], ubuf.at[src, c], u_ss.at[0, c], u_rs.at[src, c], {"mp": src}).wait_recv()

        def meet():
            with scope("barrier"):
                small_copies[0].wait()
                pl.semaphore_wait(barrier, n_cand - 1 + n_mp - 1)
            for d in range(1, n_cand):
                user_copy(d).start()
            slots[j] = user_ref[...]

        with scope("firstpart"):
            @pl.when(pool_side)
            def _():
                pool_m_copy.wait()
                from_pool(base_mp, pool_m, feat)
                stage_a(0)

        meet()

        with scope("layer1"):
            @pl.when(pool_side)
            def _():
                if low > 0:
                    scatter_copy(0, 0).start()
                for c in range(1, n1):
                    with scope(f"a{c}"):
                        stage_a(c)
                        if low > 0:
                            scatter_copy(c, 0).start()
                    with scope(f"b{c - 1}"):
                        stage_b(c - 1)
                with scope(f"b{n1 - 1}"):
                    stage_b(n1 - 1)

            @pl.when(user_side)
            def _():
                with scope("users"):
                    from_all_users()
                with scope("lhs"):
                    rows_of = [user_row(u, i, feat) for u in range(users)]
                    if users == 1:
                        lhs[...] = jnp.broadcast_to(rows_of[0], lhs.shape).astype(BF16)
                    else:
                        place = lax.broadcasted_iota(jnp.int32, lhs.shape, 0)
                        filled = jnp.zeros(lhs.shape, F32)
                        for u in range(users):
                            filled = jnp.where(place == u, rows_of[u], filled)
                        lhs[...] = filled.astype(BF16)
                for c in range(n1):
                    with scope(f"um{c}"):
                        w1_copies[c].wait()
                        term = jnp.dot(lhs[...], w1_v[c], preferred_element_type=F32)
                        ubuf[i, c] = term[0:users]
                        for d in range(1, n_mp):
                            part_copy(c, d).start()

        with scope("bases"):
            for copy in w2_copies:
                copy.start()

            @pl.when(pool_side)
            def _():
                from_all_users()

            @pl.when(user_side)
            def _():
                from_user(base_mp, i, feat)

            @pl.when(col_pool)
            def _():
                pool_c_copy.wait()
                from_pool(base_col, pool_c, col)

            @pl.when(jnp.logical_not(col_pool))
            def _():
                from_user(base_col, j, col)

            for copy in small_copies[3:]:
                copy.wait()

        def take_across(c):
            @pl.when(user_side)
            def _():
                with scope(f"across{c}"):
                    across_copy(c).wait_recv()
                spread(c)

        def first_cross(c):
            with scope(f"gw{c}"):
                for b in range(low - 1, -1, -1):
                    gather_wait(c, b)
                    if b > 0:
                        gather_copy(c, b - 1).start()
            with scope(f"pw{c}"):
                @pl.when(user_side)
                def _():
                    for d in range(1, half):
                        part_wait(c, lax.rem(i + d, half))

                @pl.when(pool_side)
                def _():
                    for src in range(half):
                        part_wait(c, src)

            cols = slice(c * cw1, (c + 1) * cw1)
            added = b1_ref[:, cols]
            for src in range(half):
                added = added + ubuf[src, c]
            for p in range(n_mp):
                r = slice(p * block, (p + 1) * block)
                u = user_of(p)
                base = base_col[r, cols].astype(F32)
                cross1[c, r, :] = (base * (psum[c, r, :].astype(F32) + added[u : u + 1]) + base).astype(BF16)

        halves = [slice(g * part, (g + 1) * part) for g in range(2)]
        toward = 1 - 2 * nd

        def z_copy(g, n, way, src, step):
            return remote(
                src.at[n, halves[g], :], zr.at[way, n, halves[g], :], z_ss.at[way, g, n], z_rs.at[way, g, n],
                {"cand": j + step},
            )

        def z_wait(g, n, way):
            remote(
                q_send.at[n, halves[g], :], zr.at[way, n, halves[g], :], z_ss.at[way, g, n], z_rs.at[way, g, n], {"cand": j}
            ).wait_recv()

        def first_out(n):
            cols = slice(n * cw2, (n + 1) * cw2)
            term = jnp.dot(cross1[n1 - 1], w2_v[(n1 - 1) * cw1 : n1 * cw1, cols], preferred_element_type=F32)
            if n1 > 1:
                term = acc2[:, cols] + term
            owner = (j == i * ratio + (n * cw2) // col).astype(F32)
            inside = (n * cw2) % col
            carried = cross1[inside // cw1, :, inside % cw1 : inside % cw1 + cw2].astype(F32)
            term = base_mp[:, cols].astype(F32) * (term + owner * b2_ref[:, cols]) + owner * carried
            q_send[n] = term.astype(BF16)

        ahead = min(3, n1)
        for c in range(ahead):
            take_across(c)
        for c in range(n1):
            first_cross(c)
            if c == 0:
                for copy in w3_copies:
                    copy.start()
            if c + ahead < n1:
                take_across(c + ahead)
            w2_copies[c].wait()
            if c < n1 - 1:
                with scope(f"l2_{c}"):
                    term = jnp.dot(cross1[c], w2_v[c * cw1 : (c + 1) * cw1, :], preferred_element_type=F32)
                    acc2[...] = term if c == 0 else acc2[...] + term
        per = min(2, n2)
        for s in range(0, n2, per):
            with scope(f"q{s}"):
                for n in range(s, min(s + per, n2)):
                    first_out(n)

                @pl.when(end)
                def _():
                    for n in range(s, min(s + per, n2)):
                        z_copy(0, n, nd, q_send, toward).start()

        @pl.when(end)
        def _():
            for n in range(n2):
                z_copy(1, n, nd, q_send, toward).start()

        def near(g, n):
            @pl.when(inner)
            def _():
                with scope(f"near{g}_{n}"):
                    z_wait(g, n, nd)
                zs[nd, n, halves[g], :] = (zr[nd, n, halves[g], :].astype(F32) + q_send[n, halves[g], :].astype(F32)).astype(BF16)
                z_copy(g, n, nd, zs.at[nd], toward).start()

        def far(g, n):
            with scope(f"far{g}_{n}"):
                z_wait(g, n, 1 - nd)

            @pl.when(inner)
            def _():
                zs[1 - nd, n, halves[g], :] = (
                    zr[1 - nd, n, halves[g], :].astype(F32) + q_send[n, halves[g], :].astype(F32)
                ).astype(BF16)
                z_copy(g, n, 1 - nd, zs.at[1 - nd], -toward).start()

        def third(g, n):
            cols = slice(n * cw2, (n + 1) * cw2)
            r = halves[g]
            value = (
                q_send[n, r, :].astype(F32) + zr[0, n, r, :].astype(F32) + zr[1, n, r, :].astype(F32)
            ).astype(BF16)
            x3[r, cols] = value
            if g == 0:
                w3_copies[n].wait()
            term = jnp.dot(value, w3_v[cols, :], preferred_element_type=F32)
            acc3[r, :] = term if n == 0 else acc3[r, :] + term

        def own_start(d):
            peer = lax.rem(i + d, n_mp)
            return peer, pl.ds(pl.multiple_of(reverse_bits(peer, bits) * block, block), block)

        def last_copy(c, d):
            peer, r = own_start(d)
            cols = slice(c * cw3, (c + 1) * cw3)
            return remote(
                send3.at[r, cols], recv3.at[i, :, cols], c_ss.at[d, c], c_rs.at[i, c], {"mp": peer}
            )

        owner3 = (i == j // ratio).astype(F32)

        def epilogue(g):
            r = halves[g]
            same = bit_of(0) == g
            lanes = jnp.zeros((part, 128), F32)
            for c in range(n3):
                cols = slice(c * cw3, (c + 1) * cw3)
                if ratio == 1:
                    carried = x3[r, cols]
                else:
                    carried = x3[r, pl.ds(pl.multiple_of(lax.rem(j, ratio) * col + c * cw3, 128), cw3)]
                term = (
                    base_col[r, cols].astype(F32) * (acc3[r, cols] + owner3 * b3_ref[:, cols])
                    + owner3 * carried.astype(F32)
                )
                acc3[r, cols] = term
                send3[r, cols] = term.astype(BF16)

                @pl.when(same)
                def _():
                    for d in range(2, n_mp, 2):
                        last_copy(c, d).start()

                @pl.when(jnp.logical_not(same))
                def _():
                    for d in range(1, n_mp, 2):
                        last_copy(c, d).start()

            for c in range(n3):
                cols = slice(c * cw3, (c + 1) * cw3)
                scored = acc3[r, cols] * score_ref[cols].astype(F32).reshape(1, cw3)
                for k in range(0, cw3, 128):
                    lanes = lanes + scored[:, k : k + 128]
            q_rows[r, :] = lanes

        events = [(g, n) for g in range(2) for n in range(n2)]
        skew = min(8, n2)
        if max(rows, 128) > rows:
            q_rows[rows:, :] = jnp.zeros((max(rows, 128) - rows, 128), F32)
        for s in range(len(events) + skew):
            if s < len(events):
                near(*events[s])
            if s < skew:
                continue
            g, n = events[s - skew]
            far(g, n)
            with scope(f"third{g}_{n}"):
                third(g, n)
            if n == n2 - 1:
                with scope(f"epi{g}"):
                    epilogue(g)

        with scope("qsend"):
            q_all[me] = jnp.sum(q_rows[...].T, axis=0, keepdims=True)

            def q_copy(d):
                peer = lax.rem(me + d, group)
                return remote(
                    q_all.at[me], q_all.at[me], q_ss.at[d], q_rs.at[me],
                    {"mp": peer // n_cand, "cand": lax.rem(peer, n_cand)},
                )

            def q_start(d, carry):
                q_copy(d).start()
                return carry

            lax.fori_loop(1, group, q_start, 0)

        mine = pl.ds(pl.multiple_of(reverse_bits(i, bits) * block, block), block)
        for c in range(n3):
            cols = slice(c * cw3, (c + 1) * cw3)
            with scope(f"last{c}"):
                for d in range(1, n_mp):
                    src = lax.rem(i - d + n_mp, n_mp)
                    remote(
                        send3.at[mine, cols], recv3.at[src, :, cols], c_ss.at[d, c], c_rs.at[src, c], {"mp": src}
                    ).wait_recv()
            term = acc3[mine, cols]
            for d in range(1, n_mp):
                term = term + recv3[lax.rem(i - d + n_mp, n_mp), :, cols].astype(F32)
            out_ref[:, cols] = term.astype(BF16)

        with scope("qwait"):
            def q_wait(d, carry):
                k = lax.rem(me - d + group, group)
                remote(q_all.at[k], q_all.at[k], q_ss.at[d], q_rs.at[k], {"cand": j}).wait_recv()
                return carry

            lax.fori_loop(1, group, q_wait, 0)
            total = jnp.sum(q_all[...], axis=0)
            for k in range(n_mp):
                p = reverse_bits(k, bits)

                @pl.when(i == k)
                def _():
                    logit_ref[...] = total[:, p * block : (p + 1) * block]

        with scope("sent"):
            for d in range(1, n_cand):
                user_copy(d).wait_send()
            for c in range(n1):
                @pl.when(pool_side)
                def _():
                    for b in range(low):
                        scatter_copy(c, b).wait_send()
                    across_copy(c).wait_send()

                @pl.when(user_side)
                def _():
                    for d in range(1, n_mp):
                        part_copy(c, d).wait_send()

                for b in range(low):
                    gather_copy(c, b).wait_send()
            for g in range(2):
                for n in range(n2):
                    z_copy(g, n, nd, q_send, toward).wait_send()

                    @pl.when(inner)
                    def _():
                        z_copy(g, n, 1 - nd, q_send, -toward).wait_send()
            for c in range(n3):
                for d in range(1, n_mp):
                    last_copy(c, d).wait_send()

            def q_sent(d, carry):
                q_copy(d).wait_send()
                return carry

            lax.fori_loop(1, group, q_sent, 0)

    return kernel


def solution(mesh):
    n_mp, n_cand = mesh.shape["mp"], mesh.shape["cand"]

    def body(
        user_feats, user_slot, cand_pool, cand_ids, first_weight, first_bias,
        second_weight, second_bias, third_weight, third_bias, score_weight,
    ):
        slots_each, half_width = user_feats.shape
        users, per_user = cand_ids.shape
        rows = users * per_user
        pool_count = cand_pool.shape[0]
        feat, col = first_weight.shape
        n1 = max(1, col // 256)
        n2 = max(1, feat // 256)
        n3 = max(1, col // 512)
        lhs_rows = -(-users // 16) * 16
        cw1, cw2 = col // n1, feat // n2
        bits = n_mp.bit_length() - 1
        low = max(1, bits - 1)
        half = n_mp // 2
        block = rows // n_mp
        group = n_mp * n_cand
        shapes = (rows, per_user, users, slots_each, half_width, pool_count, feat, col, n1, n2, n3, lhs_rows)
        vmem = pl.BlockSpec(memory_space=pltpu.VMEM)
        hbm = pl.BlockSpec(memory_space=pl.ANY)
        dma = pltpu.SemaphoreType.DMA
        crossed, logits = pl.pallas_call(
            make_kernel(n_mp, n_cand, shapes),
            out_shape=(
                pltpu.VMEM((block, col), BF16),
                pltpu.VMEM((1, block), F32),
            ),
            in_specs=[hbm] * 11,
            out_specs=(vmem, vmem),
            scratch_shapes=[
                pltpu.SMEM((users,), jnp.int32),
                pltpu.VMEM((slots_each, half_width), BF16),
                pltpu.VMEM((users, per_user), jnp.int32),
                pltpu.VMEM((1, col), F32),
                pltpu.VMEM((1, feat), F32),
                pltpu.VMEM((1, col), F32),
                pltpu.VMEM((col,), BF16),
                dma((7,)),
                pltpu.VMEM((n_cand, slots_each, half_width), BF16),
                pltpu.VMEM((pool_count, feat), BF16),
                pltpu.VMEM((pool_count, col), BF16),
                pltpu.VMEM((n1, feat, cw1), BF16),
                pltpu.VMEM((col, feat), BF16),
                pltpu.VMEM((feat, col), BF16),
                pltpu.VMEM((rows, pool_count), BF16),
                pltpu.VMEM((rows, feat), BF16),
                pltpu.VMEM((rows, col), BF16),
                pltpu.VMEM((lhs_rows, feat), BF16),
                pltpu.VMEM((n1, rows, cw1), F32),
                pltpu.VMEM((n1, rows, cw1), BF16),
                pltpu.VMEM((low, n1, rows // 2, cw1), BF16),
                pltpu.VMEM((n1, rows, cw1), BF16),
                pltpu.VMEM((half, n1, users, cw1), F32),
                pltpu.VMEM((n1, rows, cw1), BF16),
                pltpu.VMEM((rows, feat), F32),
                pltpu.VMEM((n2, rows, cw2), BF16),
                pltpu.VMEM((2, n2, rows, cw2), BF16),
                pltpu.VMEM((2, n2, rows, cw2), BF16),
                pltpu.VMEM((rows, feat), BF16),
                pltpu.VMEM((rows, col), F32),
                pltpu.VMEM((rows, col), BF16),
                pltpu.VMEM((n_mp, block, col), BF16),
                pltpu.VMEM((max(rows, 128), 128), F32),
                pltpu.VMEM((group, 1, max(rows, 128)), F32),
                dma((2 + 2 * n1 + n2,)),
                dma((n_cand,)),
                dma((n_cand,)),
                dma((low, n1)),
                dma((low, n1)),
                dma((n1,)),
                dma((n1,)),
                dma((low, n1)),
                dma((low, n1)),
                dma((n_mp, n1)),
                dma((half, n1)),
                dma((2, 2, n2)),
                dma((2, 2, n2)),
                dma((n_mp, n3)),
                dma((n_mp, n3)),
                dma((group,)),
                dma((group,)),
            ],
            compiler_params=pltpu.CompilerParams(
                collective_id=0, has_side_effects=True, vmem_limit_bytes=67043328 - 3000 * 1024
            ),
        )(
            user_feats, user_slot, cand_pool, cand_ids, first_weight, first_bias.reshape(1, -1),
            second_weight, second_bias.reshape(1, -1), third_weight, third_bias.reshape(1, -1),
            score_weight,
        )
        crossed, logits = pl.pallas_call(
            hand_on,
            out_shape=(
                jax.ShapeDtypeStruct((block, col), BF16),
                jax.ShapeDtypeStruct((1, block), F32),
            ),
            in_specs=[vmem, vmem],
            out_specs=(hbm, hbm),
            scratch_shapes=[dma((2,))],
            compiler_params=pltpu.CompilerParams(vmem_limit_bytes=1024 * 1024),
        )(crossed, logits)
        return crossed, logits.reshape(-1)

    in_specs = (
        P(("groups", "cand"), None),
        P("groups"),
        P("groups", None),
        P("groups", None),
        P("mp", "cand"),
        P("cand"),
        P("cand", "mp"),
        P("mp"),
        P("mp", "cand"),
        P("cand"),
        P("cand"),
    )
    out_specs = (P(("groups", "mp"), "cand"), P(("groups", "mp")))
    return jax.shard_map(body, mesh=mesh, in_specs=in_specs, out_specs=out_specs, check_vma=False)
```

time: 40 us -> 38.4 us (0.960)
  Pallas kernels: 38.4 us -> 36.9 us
    pallas_call x1, Pallas kernels: 37.8 us -> 36.3 us  [body(): pl.pallas_call(make_kernel(n_mp, n_cand, shapes), out_shape=(pltpu.VMEM((...]
where the time goes in v1:
time: 38.4 us; the launch traced here: 38.2 us
  Pallas kernels  36.9 us (96%)
  between operations  1.29 us (3%)
    pallas_call x1, Pallas kernels, body(): pl.pallas_call(make_kernel(n_mp, n_cand, shapes), out_shape=(pltpu.VMEM((...  36.3 us

profile of v1, /device:TPU:0, one launch (start us, length us, event | category | flops | bytes accessed | tf_op | source)
XLA Modules:
  0.0 38.2 jit_solution(17756592889265292704)
XLA Ops:
  1.3 36.3 %shard_map.122 = (bf16[16,2048]{1,0:T(8,128)(2,1)S(1)}, f32[1,16]{1,0:T(1,128)S(1)}) custom-call(bf16[1,4096]{1,0:T(2,128)(2,1)} %user_hbm.1, s32[1]{0:T(128)S(6)} %copy.13.slot_hbm, bf16[256,4096]{1,0:T(8,128)(2,1)} %pool_hbm.1, s32[1,64]{1,0:T(1,128)} %ids_hbm.1, bf16[2048,2048]{1,0:T(8,128)(2,1)} %w1_hbm.1, f32[1,2048]{1,0:T(1,128)} %bitcast.4, ...), custom_call_target="tpu_custom_call" | custom-call | tf_op jit(solution)/shard_map/pallas_call | solution.py:618
  37.6 0.7 %shard_map.123 = (bf16[16,2048]{1,0:T(8,128)(2,1)}, f32[1,16]{1,0:T(1,128)}) custom-call(bf16[16,2048]{1,0:T(8,128)(2,1)S(1)} %get-tuple-element.6.crossed_ref, f32[1,16]{1,0:T(1,128)S(1)} %get-tuple-element.7.logit_ref), custom_call_target="tpu_custom_call" | custom-call | tf_op jit(solution)/shard_map/pallas_call | solution.py:687

commit v2 on v1

--- a/solution.py
+++ b/solution.py
@@ -53,15 +53,14 @@
     def kernel(
         user_hbm, slot_hbm, pool_hbm, ids_hbm, w1_hbm, b1_hbm, w2_hbm, b2_hbm, w3_hbm, b3_hbm, score_hbm,
         out_ref, logit_ref,
-        slot_ref, user_ref, ids_ref, b1_ref, b2_ref, b3_ref, score_ref, small_sem, slots, pool_m, pool_c, w1_v, w2_v, w3_v,
+        slot_ref, ids_ref, b1_ref, b2_ref, b3_ref, score_ref, small_sem, slots, pool_m, pool_c, w1_v, w2_v, w3_v,
         onehot, base_mp, base_col, lhs, acc1, send1, recv1, psum, ubuf, cross1, acc2, q_send, zr, zs, x3, acc3, send3, recv3,
         q_rows, q_all,
-        w_sem, user_ss, user_rs, a_ss, a_rs, x_ss, x_rs, g_ss, g_rs, u_ss, u_rs, z_ss, z_rs, c_ss, c_rs, q_ss, q_rs,
+        w_sem, user_sem, a_ss, a_rs, x_ss, x_rs, g_ss, g_rs, u_ss, u_rs, z_ss, z_rs, c_ss, c_rs, q_sem,
     ):
         i = lax.axis_index("mp")
         j = lax.axis_index("cand")
         me = i * n_cand + j
-        pending = []
         user_side = i < half
         pool_side = jnp.logical_not(user_side)
 
@@ -84,7 +83,7 @@
             pltpu.make_async_copy(src, dst, small_sem.at[k])
             for k, (src, dst) in enumerate(
                 (
-                    (user_hbm, user_ref), (ids_hbm, ids_ref), (slot_hbm, slot_ref), (b1_hbm, b1_ref),
+                    (ids_hbm, ids_ref), (slot_hbm, slot_ref), (user_hbm, slots.at[j]), (b1_hbm, b1_ref),
                     (b2_hbm, b2_ref), (b3_hbm, b3_ref), (score_hbm, score_ref),
                 )
             )
@@ -96,14 +95,8 @@
         w1_copies = [
             pltpu.make_async_copy(w1_hbm.at[:, pl.ds(c * cw1, cw1)], w1_v.at[c], w_sem.at[2 + c]) for c in range(n1)
         ]
-        w2_copies = [
-            pltpu.make_async_copy(w2_hbm.at[pl.ds(c * cw1, cw1), :], w2_v.at[pl.ds(c * cw1, cw1), :], w_sem.at[2 + n1 + c])
-            for c in range(n1)
-        ]
-        w3_copies = [
-            pltpu.make_async_copy(w3_hbm.at[pl.ds(c * cw2, cw2), :], w3_v.at[pl.ds(c * cw2, cw2), :], w_sem.at[2 + 2 * n1 + c])
-            for c in range(n2)
-        ]
+        w2_copy = pltpu.make_async_copy(w2_hbm, w2_v, w_sem.at[2 + n1])
+        w3_copy = pltpu.make_async_copy(w3_hbm, w3_v, w_sem.at[3 + n1])
         col_pool = j >= first_pool_col
         with scope("loads"):
             for copy in small_copies[:3]:
@@ -122,6 +115,10 @@
             def _():
                 pool_c_copy.start()
 
+            @pl.when(user_side)
+            def _():
+                w2_copy.start()
+
             end = jnp.logical_or(j == 0, j == n_cand - 1)
             inner = jnp.logical_not(end)
             nd = (j >= (n_cand + 1) // 2).astype(jnp.int32)
@@ -130,17 +127,18 @@
             def _():
                 zr[nd] = jnp.zeros(zr.shape[1:], BF16)
 
-        with scope("onehot"):
-            small_copies[1].wait()
-            for u in range(users):
-                hot = (
-                    lax.broadcasted_iota(jnp.int32, (pool_count, per_user), 0) == ids_ref[u : u + 1, :]
-                ).astype(F32).T
-                for p in range(n_mp):
-                    first = reverse_bits(p, bits) * block
-                    if first // per_user == u:
-                        off = first % per_user
-                        onehot[p * block : (p + 1) * block, :] = hot[off : off + block].astype(BF16)
+        def build_onehot():
+            with scope("onehot"):
+                small_copies[0].wait()
+                for u in range(users):
+                    hot = (
+                        lax.broadcasted_iota(jnp.int32, (pool_count, per_user), 0) == ids_ref[u : u + 1, :]
+                    ).astype(F32).T
+                    for p in range(n_mp):
+                        first = reverse_bits(p, bits) * block
+                        if first // per_user == u:
+                            off = first % per_user
+                            onehot[p * block : (p + 1) * block, :] = hot[off : off + block].astype(BF16)
 
         def from_pool(dst, src, width):
             for c in range(0, width, 256):
@@ -148,7 +146,7 @@
 
         def user_row(u, index, width):
             start = pl.multiple_of(index * width, 128)
-            slot = slot_ref[u]
+            slot = slot_ref[0, u]
             row = slots[slot // slots_each, :, pl.ds(start, width)].astype(F32)
             if slots_each > 1:
                 pick = lax.broadcasted_iota(jnp.int32, row.shape, 0) == lax.rem(slot, slots_each)
@@ -161,12 +159,13 @@
                 dst[p * block : (p + 1) * block, :] = jnp.broadcast_to(rows_of[user_of(p)], (block, width)).astype(BF16)
 
         def user_copy(d):
-            return remote(user_ref, slots.at[j], user_ss.at[d - 1], user_rs.at[j], {"cand": lax.rem(j + d, n_cand)})
+            return remote(user_hbm, slots.at[j], user_sem.at[0], user_sem.at[1], {"cand": lax.rem(j + d, n_cand)})
+
+        others = slots.at[pl.ds(0, n_cand - 1)]
 
         def from_all_users():
-            for d in range(1, n_cand):
-                k = lax.rem(j - d + n_cand, n_cand)
-                remote(user_ref, slots.at[k], user_ss.at[d - 1], user_rs.at[k], {"cand": k}).wait_recv()
+            remote(others, others, user_sem.at[0], user_sem.at[1], {"cand": j}).wait_recv()
+            small_copies[1].wait()
             small_copies[2].wait()
 
         def bit_of(b):
@@ -193,22 +192,22 @@
         def scatter_copy(c, b):
             size = rows >> (b + 1)
             return remote(
-                send1.at[c, other(b), :], recv1.at[b, c, pl.ds(0, size), :], a_ss.at[b, c], a_rs.at[b, c], {"mp": partner(b)}
+                send1.at[c, other(b), :], recv1.at[b, c, pl.ds(0, size), :], a_ss.at[b], a_rs.at[b, c], {"mp": partner(b)}
             )
 
         def across_copy(c):
             return remote(
-                psum.at[c, seg(low), :], psum.at[c, seg(low), :], x_ss.at[c], x_rs.at[c], {"mp": lax.rem(i + half, n_mp)}
+                psum.at[c, seg(low), :], psum.at[c, seg(low), :], x_ss.at[0], x_rs.at[c], {"mp": lax.rem(i + half, n_mp)}
             )
 
         def gather_copy(c, b):
             return remote(
-                psum.at[c, seg(b + 1), :], psum.at[c, seg(b + 1), :], g_ss.at[b, c], g_rs.at[b, c], {"mp": partner(b)}
+                psum.at[c, seg(b + 1), :], psum.at[c, seg(b + 1), :], g_ss.at[b], g_rs.at[b, c], {"mp": partner(b)}
             )
 
         def gather_wait(c, b):
             remote(
-                psum.at[c, other(b), :], psum.at[c, other(b), :], g_ss.at[b, c], g_rs.at[b, c], {"mp": partner(b)}
+                psum.at[c, other(b), :], psum.at[c, other(b), :], g_ss.at[b], g_rs.at[b, c], {"mp": partner(b)}
             ).wait_recv()
 
         def spread(c):
@@ -239,27 +238,23 @@
             spread(c)
 
         def part_copy(c, d):
-            return remote(ubuf.at[i, c], ubuf.at[i, c], u_ss.at[d, c], u_rs.at[i, c], {"mp": lax.rem(i + d, n_mp)})
+            return remote(ubuf.at[i, c], ubuf.at[i, c], u_ss.at[d], u_rs.at[i, c], {"mp": lax.rem(i + d, n_mp)})
 
         def part_wait(c, src):
-            remote(ubuf.at[src, c], ubuf.at[src, c], u_ss.at[0, c], u_rs.at[src, c], {"mp": src}).wait_recv()
-
-        def meet():
-            with scope("barrier"):
-                small_copies[0].wait()
-                pl.semaphore_wait(barrier, n_cand - 1 + n_mp - 1)
-            for d in range(1, n_cand):
-                user_copy(d).start()
-            slots[j] = user_ref[...]
+            remote(ubuf.at[src, c], ubuf.at[src, c], u_ss.at[0], u_rs.at[src, c], {"mp": src}).wait_recv()
 
         with scope("firstpart"):
             @pl.when(pool_side)
             def _():
+                build_onehot()
                 pool_m_copy.wait()
                 from_pool(base_mp, pool_m, feat)
                 stage_a(0)
 
-        meet()
+        with scope("barrier"):
+            pl.semaphore_wait(barrier, n_cand - 1 + n_mp - 1)
+        for d in range(1, n_cand):
+            user_copy(d).start()
 
         with scope("layer1"):
             @pl.when(pool_side)
@@ -273,6 +268,7 @@
                             scatter_copy(c, 0).start()
                     with scope(f"b{c - 1}"):
                         stage_b(c - 1)
+                w2_copy.start()
                 with scope(f"b{n1 - 1}"):
                     stage_b(n1 - 1)
 
@@ -290,17 +286,17 @@
                         for u in range(users):
                             filled = jnp.where(place == u, rows_of[u], filled)
                         lhs[...] = filled.astype(BF16)
-                for c in range(n1):
-                    with scope(f"um{c}"):
-                        w1_copies[c].wait()
+                with scope("um"):
+                    for copy in w1_copies:
+                        copy.wait()
+                    for c in range(n1):
                         term = jnp.dot(lhs[...], w1_v[c], preferred_element_type=F32)
                         ubuf[i, c] = term[0:users]
-                        for d in range(1, n_mp):
+                        for d in range(n_mp - 1, 0, -1):
                             part_copy(c, d).start()
 
         with scope("bases"):
-            for copy in w2_copies:
-                copy.start()
+            w3_copy.start()
 
             @pl.when(pool_side)
             def _():
@@ -309,6 +305,14 @@
             @pl.when(user_side)
             def _():
                 from_user(base_mp, i, feat)
+
+                @pl.when(col_pool)
+                def _():
+                    build_onehot()
+
+                @pl.when(jnp.logical_not(col_pool))
+                def _():
+                    small_copies[0].wait()
 
             @pl.when(col_pool)
             def _():
@@ -361,13 +365,13 @@
 
         def z_copy(g, n, way, src, step):
             return remote(
-                src.at[n, halves[g], :], zr.at[way, n, halves[g], :], z_ss.at[way, g, n], z_rs.at[way, g, n],
+                src.at[n, halves[g], :], zr.at[way, n, halves[g], :], z_ss.at[way], z_rs.at[way, g, n],
                 {"cand": j + step},
             )
 
         def z_wait(g, n, way):
             remote(
-                q_send.at[n, halves[g], :], zr.at[way, n, halves[g], :], z_ss.at[way, g, n], z_rs.at[way, g, n], {"cand": j}
+                q_send.at[n, halves[g], :], zr.at[way, n, halves[g], :], z_ss.at[way], z_rs.at[way, g, n], {"cand": j}
             ).wait_recv()
 
         def first_out(n):
@@ -386,12 +390,10 @@
             take_across(c)
         for c in range(n1):
             first_cross(c)
-            if c == 0:
-                for copy in w3_copies:
-                    copy.start()
             if c + ahead < n1:
                 take_across(c + ahead)
-            w2_copies[c].wait()
+            if c == 0:
+                w2_copy.wait()
             if c < n1 - 1:
                 with scope(f"l2_{c}"):
                     term = jnp.dot(cross1[c], w2_v[c * cw1 : (c + 1) * cw1, :], preferred_element_type=F32)
@@ -438,8 +440,8 @@
                 q_send[n, r, :].astype(F32) + zr[0, n, r, :].astype(F32) + zr[1, n, r, :].astype(F32)
             ).astype(BF16)
             x3[r, cols] = value
-            if g == 0:
-                w3_copies[n].wait()
+            if g == 0 and n == 0:
+                w3_copy.wait()
             term = jnp.dot(value, w3_v[cols, :], preferred_element_type=F32)
             acc3[r, :] = term if n == 0 else acc3[r, :] + term
 
@@ -451,7 +453,7 @@
             peer, r = own_start(d)
             cols = slice(c * cw3, (c + 1) * cw3)
             return remote(
-                send3.at[r, cols], recv3.at[i, :, cols], c_ss.at[d, c], c_rs.at[i, c], {"mp": peer}
+                send3.at[r, cols], recv3.at[i, :, cols], c_ss.at[0], c_rs.at[c], {"mp": peer}
             )
 
         owner3 = (i == j // ratio).astype(F32)
@@ -513,7 +515,7 @@
             def q_copy(d):
                 peer = lax.rem(me + d, group)
                 return remote(
-                    q_all.at[me], q_all.at[me], q_ss.at[d], q_rs.at[me],
+                    q_all.at[me], q_all.at[me], q_sem.at[0], q_sem.at[1],
                     {"mp": peer // n_cand, "cand": lax.rem(peer, n_cand)},
                 )
 
@@ -527,23 +529,16 @@
         for c in range(n3):
             cols = slice(c * cw3, (c + 1) * cw3)
             with scope(f"last{c}"):
-                for d in range(1, n_mp):
-                    src = lax.rem(i - d + n_mp, n_mp)
-                    remote(
-                        send3.at[mine, cols], recv3.at[src, :, cols], c_ss.at[d, c], c_rs.at[src, c], {"mp": src}
-                    ).wait_recv()
+                came = recv3.at[pl.ds(0, n_mp - 1), :, cols]
+                remote(came, came, c_ss.at[0], c_rs.at[c], {"mp": i}).wait_recv()
             term = acc3[mine, cols]
             for d in range(1, n_mp):
                 term = term + recv3[lax.rem(i - d + n_mp, n_mp), :, cols].astype(F32)
             out_ref[:, cols] = term.astype(BF16)
 
         with scope("qwait"):
-            def q_wait(d, carry):
-                k = lax.rem(me - d + group, group)
-                remote(q_all.at[k], q_all.at[k], q_ss.at[d], q_rs.at[k], {"cand": j}).wait_recv()
-                return carry
-
-            lax.fori_loop(1, group, q_wait, 0)
+            rest = q_all.at[pl.ds(0, group - 1)]
+            remote(rest, rest, q_sem.at[0], q_sem.at[1], {"cand": j}).wait_recv()
             total = jnp.sum(q_all[...], axis=0)
             for k in range(n_mp):
                 p = reverse_bits(k, bits)
@@ -552,39 +547,33 @@
                 def _():
                     logit_ref[...] = total[:, p * block : (p + 1) * block]
 
+        def sent(ref, sem):
+            remote(ref, ref, sem, sem, {"cand": j}).wait_send()
+
         with scope("sent"):
-            for d in range(1, n_cand):
-                user_copy(d).wait_send()
-            for c in range(n1):
-                @pl.when(pool_side)
-                def _():
-                    for b in range(low):
-                        scatter_copy(c, b).wait_send()
-                    across_copy(c).wait_send()
-
-                @pl.when(user_side)
-                def _():
-                    for d in range(1, n_mp):
-                        part_copy(c, d).wait_send()
-
+            sent(others, user_sem.at[0])
+
+            @pl.when(pool_side)
+            def _():
                 for b in range(low):
-                    gather_copy(c, b).wait_send()
-            for g in range(2):
-                for n in range(n2):
-                    z_copy(g, n, nd, q_send, toward).wait_send()
-
-                    @pl.when(inner)
-                    def _():
-                        z_copy(g, n, 1 - nd, q_send, -toward).wait_send()
-            for c in range(n3):
+                    sent(recv1.at[b, :, pl.ds(0, rows >> (b + 1)), :], a_ss.at[b])
+                sent(psum.at[:, seg(low), :], x_ss.at[0])
+
+            @pl.when(user_side)
+            def _():
                 for d in range(1, n_mp):
-                    last_copy(c, d).wait_send()
-
-            def q_sent(d, carry):
-                q_copy(d).wait_send()
-                return carry
-
-            lax.fori_loop(1, group, q_sent, 0)
+                    sent(ubuf.at[i], u_ss.at[d])
+
+            for b in range(low):
+                sent(psum.at[:, seg(b + 1), :], g_ss.at[b])
+            sent(q_send, z_ss.at[nd])
+
+            @pl.when(inner)
+            def _():
+                sent(q_send, z_ss.at[1 - nd])
+
+            sent(recv3.at[pl.ds(0, n_mp - 1)], c_ss.at[0])
+            sent(rest, q_sem.at[0])
 
     return kernel
 
@@ -601,7 +590,7 @@
         rows = users * per_user
         pool_count = cand_pool.shape[0]
         feat, col = first_weight.shape
-        n1 = max(1, col // 256)
+        n1 = max(1, col // 512)
         n2 = max(1, feat // 256)
         n3 = max(1, col // 512)
         lhs_rows = -(-users // 16) * 16
@@ -624,8 +613,7 @@
             in_specs=[hbm] * 11,
             out_specs=(vmem, vmem),
             scratch_shapes=[
-                pltpu.SMEM((users,), jnp.int32),
-                pltpu.VMEM((slots_each, half_width), BF16),
+                pltpu.SMEM((1, users), jnp.int32),
                 pltpu.VMEM((users, per_user), jnp.int32),
                 pltpu.VMEM((1, col), F32),
                 pltpu.VMEM((1, feat), F32),
@@ -658,29 +646,27 @@
                 pltpu.VMEM((n_mp, block, col), BF16),
                 pltpu.VMEM((max(rows, 128), 128), F32),
                 pltpu.VMEM((group, 1, max(rows, 128)), F32),
-                dma((2 + 2 * n1 + n2,)),
-                dma((n_cand,)),
-                dma((n_cand,)),
+                dma((4 + n1,)),
+                dma((2,)),
+                dma((low,)),
                 dma((low, n1)),
+                dma((1,)),
+                dma((n1,)),
+                dma((low,)),
                 dma((low, n1)),
-                dma((n1,)),
-                dma((n1,)),
-                dma((low, n1)),
-                dma((low, n1)),
-                dma((n_mp, n1)),
+                dma((n_mp,)),
                 dma((half, n1)),
+                dma((2,)),
                 dma((2, 2, n2)),
-                dma((2, 2, n2)),
-                dma((n_mp, n3)),
-                dma((n_mp, n3)),
-                dma((group,)),
-                dma((group,)),
+                dma((1,)),
+                dma((n3,)),
+                dma((2,)),
             ],
             compiler_params=pltpu.CompilerParams(
                 collective_id=0, has_side_effects=True, vmem_limit_bytes=67043328 - 3000 * 1024
             ),
         )(
-            user_feats, user_slot, cand_pool, cand_ids, first_weight, first_bias.reshape(1, -1),
+            user_feats, user_slot.reshape(1, -1), cand_pool, cand_ids, first_weight, first_bias.reshape(1, -1),
             second_weight, second_bias.reshape(1, -1), third_weight, third_bias.reshape(1, -1),
             score_weight,
         )

time: 38.4 us -> 34.6 us (0.901)
  Pallas kernels: 36.9 us -> 33.2 us
    pallas_call x1, Pallas kernels: 36.3 us -> 32.5 us  [body(): pl.pallas_call(make_kernel(n_mp, n_cand, shapes), out_shape=(pltpu.VMEM((...]
where the time goes in v2:
time: 34.6 us; the launch traced here: 34.4 us
  Pallas kernels  33.2 us (96%)
  between operations  1.29 us (4%)
    pallas_call x1, Pallas kernels, body(): pl.pallas_call(make_kernel(n_mp, n_cand, shapes), out_shape=(pltpu.VMEM((...  32.5 us

profile of v2, /device:TPU:0, one launch (start us, length us, event | category | flops | bytes accessed | tf_op | source)
XLA Modules:
  0.0 34.4 jit_solution(11088151873866031505)
XLA Ops:
  1.3 32.5 %shard_map.122 = (bf16[16,2048]{1,0:T(8,128)(2,1)S(1)}, f32[1,16]{1,0:T(1,128)S(1)}) custom-call(bf16[1,4096]{1,0:T(2,128)(2,1)} %user_hbm.1, s32[1,1]{1,0:T(1,128)} %bitcast.5.slot_hbm, bf16[256,4096]{1,0:T(8,128)(2,1)} %pool_hbm.1, s32[1,64]{1,0:T(1,128)} %ids_hbm.1, bf16[2048,2048]{1,0:T(8,128)(2,1)} %w1_hbm.1, f32[1,2048]{1,0:T(1,128)} %bitcast.6, ...), custom_call_target="tpu_custom_call" | custom-call | tf_op jit(solution)/shard_map/pallas_call | solution.py:607
  33.8 0.7 %shard_map.123 = (bf16[16,2048]{1,0:T(8,128)(2,1)}, f32[1,16]{1,0:T(1,128)}) custom-call(bf16[16,2048]{1,0:T(8,128)(2,1)S(1)} %get-tuple-element.6.crossed_ref, f32[1,16]{1,0:T(1,128)S(1)} %get-tuple-element.7.logit_ref), custom_call_target="tpu_custom_call" | custom-call | tf_op jit(solution)/shard_map/pallas_call | solution.py:673

commit v3 on v2

v3 whole, which is shorter than its diff:
```python
import contextlib

import jax
import jax.numpy as jnp
from jax import lax
from jax.experimental import pallas as pl
from jax.experimental.pallas import tpu as pltpu
from jax.sharding import PartitionSpec as P

MESH = pl.DeviceIdType.MESH
F32 = jnp.float32
BF16 = jnp.bfloat16


def scope(name):
    return contextlib.nullcontext()


def hand_on(crossed_ref, logit_ref, crossed_hbm, logit_hbm, sem):
    copies = [
        pltpu.make_async_copy(crossed_ref, crossed_hbm, sem.at[0]),
        pltpu.make_async_copy(logit_ref, logit_hbm, sem.at[1]),
    ]
    for copy in copies:
        copy.start()
    for copy in copies:
        copy.wait()


def make_kernel(n_mp, n_cand, shapes):
    rows, per_user, users, slots_each, half_width, pool_count, feat, col, cuts, ucuts, zcuts, n3 = shapes
    cw3 = col // n3
    n1 = len(cuts)
    bits = n_mp.bit_length() - 1
    low = bits - 1
    half = n_mp // 2
    block = rows // n_mp
    ratio = feat // col
    group = n_mp * n_cand
    part = rows // 2
    q_width = max(part, 128)
    first_pool_col = half_width // col

    def user_of(p):
        return (p * block) // per_user

    def kernel(
        user_hbm, slot_hbm, pool_hbm, ids_hbm, w1_hbm, b1_hbm, w2_hbm, b2_hbm, w3_hbm, b3_hbm, score_hbm,
        out_ref, logit_ref,
        slot_ref, ids_ref, b1_ref, b2_ref, b3_ref, score_ref, small_sem, slots, ucol, pool_m, pool_c, w1_v, w2_v, w3_v,
        onehot, base_mp, base_col, lhs, acc1, send1, recv1, psum, ubuf, cross1, acc2, q_send, zr, zs, x3, acc3, send3, recv3,
        q_rows, q_mine, q_all,
        w_sem, user_sem, ucol_sem, ready, a_ss, a_rs, x_ss, x_rs, g_ss, g_rs, u_ss, u_rs, z_ss, z_rs, c_ss, c_rs, q_sem,
    ):
        i = lax.axis_index("mp")
        j = lax.axis_index("cand")
        me = i * n_cand + j
        user_side = i < half
        pool_side = jnp.logical_not(user_side)

        def remote(src, dst, ss, rs, where):
            return pltpu.make_async_remote_copy(
                src_ref=src, dst_ref=dst, send_sem=ss, recv_sem=rs, device_id=where, device_id_type=MESH
            )

        barrier = pltpu.get_barrier_semaphore()
        with scope("greet"):
            def greet(d, carry):
                pl.semaphore_signal(barrier, inc=1, device_id={"cand": lax.rem(j + d, n_cand)}, device_id_type=MESH)
                return carry

            @pl.when(user_side)
            def _():
                lax.fori_loop(1, n_cand, greet, 0, unroll=n_cand <= 4)
                for d in range(1, n_mp):
                    pl.semaphore_signal(barrier, inc=1, device_id={"mp": lax.rem(i + d, n_mp)}, device_id_type=MESH)

            @pl.when(pool_side)
            def _():
                for d in range(1, half):
                    pl.semaphore_signal(
                        barrier, inc=1, device_id={"mp": half + lax.rem(i + d, half)}, device_id_type=MESH
                    )

                @pl.when(j > 0)
                def _():
                    pl.semaphore_signal(barrier, inc=1, device_id={"cand": j - 1}, device_id_type=MESH)

                @pl.when(j < n_cand - 1)
                def _():
                    pl.semaphore_signal(barrier, inc=1, device_id={"cand": j + 1}, device_id_type=MESH)

        small_copies = [
            pltpu.make_async_copy(src, dst, small_sem.at[k])
            for k, (src, dst) in enumerate(
                (
                    (ids_hbm, ids_ref), (slot_hbm, slot_ref), (user_hbm, slots.at[j]), (b1_hbm, b1_ref),
                    (b2_hbm, b2_ref), (b3_hbm, b3_ref), (score_hbm, score_ref),
                )
            )
        ]
        m_start = pl.multiple_of(jnp.maximum(i - half, 0) * feat, 128)
        c_start = pl.multiple_of(jnp.maximum(j - first_pool_col, 0) * col, 128)
        pool_m_copy = pltpu.make_async_copy(pool_hbm.at[:, pl.ds(m_start, feat)], pool_m, w_sem.at[0])
        pool_c_copy = pltpu.make_async_copy(pool_hbm.at[:, pl.ds(c_start, col)], pool_c, w_sem.at[1])
        w1_copies = [
            pltpu.make_async_copy(w1_hbm.at[:, cut], w1_v.at[:, cut], w_sem.at[2 + c]) for c, cut in enumerate(cuts)
        ]
        w2_copy = pltpu.make_async_copy(w2_hbm, w2_v, w_sem.at[2 + n1])
        w3_copy = pltpu.make_async_copy(w3_hbm, w3_v, w_sem.at[3 + n1])
        col_pool = j >= first_pool_col
        with scope("loads"):
            for copy in small_copies[:3]:
                copy.start()

            @pl.when(pool_side)
            def _():
                pool_m_copy.start()

            for copy in w1_copies:
                copy.start()
            for copy in small_copies[3:]:
                copy.start()

            @pl.when(col_pool)
            def _():
                pool_c_copy.start()

            @pl.when(user_side)
            def _():
                w2_copy.start()

            end = jnp.logical_or(j == 0, j == n_cand - 1)
            inner = jnp.logical_not(end)
            nd = (j >= (n_cand + 1) // 2).astype(jnp.int32)

            @pl.when(end)
            def _():
                zr[nd] = jnp.zeros(zr.shape[1:], BF16)

        def build_onehot():
            with scope("onehot"):
                small_copies[0].wait()
                for u in range(users):
                    hot = (
                        lax.broadcasted_iota(jnp.int32, (pool_count, per_user), 0) == ids_ref[u : u + 1, :]
                    ).astype(F32).T
                    for p in range(n_mp):
                        first = p * block
                        if first // per_user == u:
                            off = first % per_user
                            onehot[p * block : (p + 1) * block, :] = hot[off : off + block].astype(BF16)

        def from_pool(dst, src, width):
            for c in range(0, width, 256):
                dst[:, c : c + 256] = jnp.dot(onehot[...], src[:, c : c + 256], preferred_element_type=F32).astype(BF16)

        def user_row(u, index, width):
            start = pl.multiple_of(index * width, 128)
            slot = slot_ref[0, u]
            row = slots[slot // slots_each, :, pl.ds(start, width)].astype(F32)
            if slots_each > 1:
                pick = lax.broadcasted_iota(jnp.int32, row.shape, 0) == lax.rem(slot, slots_each)
                row = jnp.sum(jnp.where(pick, row, 0.0), axis=0, keepdims=True)
            return row

        def from_user(dst, index, width):
            rows_of = [user_row(u, index, width) for u in range(users)]
            for p in range(n_mp):
                dst[p * block : (p + 1) * block, :] = jnp.broadcast_to(rows_of[user_of(p)], (block, width)).astype(BF16)

        def user_copy(k):
            d = jnp.where(j < n_cand // 2, n_cand - k, k)
            return remote(user_hbm, slots.at[j], user_sem.at[0], user_sem.at[1], {"cand": lax.rem(j + d, n_cand)})

        def ucol_copy():
            return remote(ucol, ucol, ucol_sem.at[0], ucol_sem.at[1], {"mp": lax.rem(i + half, n_mp)})

        others = slots.at[pl.ds(0, n_cand - 1)]

        def from_all_users():
            remote(others, others, user_sem.at[0], user_sem.at[1], {"cand": j}).wait_recv()
            small_copies[1].wait()

        def bit_of(b):
            return lax.rem(i // (1 << b), 2)

        def partner(b):
            return i + (1 << b) * (1 - 2 * bit_of(b))

        lows = [0]
        for b in range(bits):
            lows.append(lows[b] + bit_of(b) * (rows >> (b + 1)))

        def seg(b):
            size = rows >> b
            if b == 0:
                return pl.ds(0, rows)
            return pl.ds(pl.multiple_of(lows[b], size), size)

        def other(b):
            size = rows >> (b + 1)
            start = lows[b] + (1 - bit_of(b)) * size
            return pl.ds(pl.multiple_of(start, size), size)

        def scatter_copy(c, b):
            size = rows >> (b + 1)
            return remote(
                send1.at[other(b), cuts[c]], recv1.at[b, pl.ds(0, size), cuts[c]], a_ss.at[b], a_rs.at[b, c], {"mp": partner(b)}
            )

        def across_copy(c):
            return remote(
                psum.at[seg(low), cuts[c]], psum.at[seg(low), cuts[c]], x_ss.at[0], x_rs.at[c], {"mp": lax.rem(i + half, n_mp)}
            )

        def gather_copy(c, b):
            return remote(
                psum.at[seg(b + 1), cuts[c]], psum.at[seg(b + 1), cuts[c]], g_ss.at[b], g_rs.at[b, c], {"mp": partner(b)}
            )

        def gather_wait(c, b):
            remote(
                psum.at[other(b), cuts[c]], psum.at[other(b), cuts[c]], g_ss.at[b], g_rs.at[b, c], {"mp": partner(b)}
            ).wait_recv()

        def spread(c):
            if low > 0:
                gather_copy(c, low - 1).start()

        def stage_a(c):
            w1_copies[c].wait()
            term = jnp.dot(base_mp[...], w1_v[:, cuts[c]], preferred_element_type=F32)
            if low > 0:
                acc1[:, cuts[c]] = term
                send1[:, cuts[c]] = term.astype(BF16)
            else:
                psum[:, cuts[c]] = term.astype(BF16)

        def stage_b(c):
            for b in range(low):
                scatter_copy(c, b).wait_recv()
                size = rows >> (b + 1)
                term = acc1[seg(b + 1), cuts[c]] + recv1[b, 0:size, cuts[c]].astype(F32)
                if b + 1 < low:
                    acc1[seg(b + 1), cuts[c]] = term
                    send1[seg(b + 1), cuts[c]] = term.astype(BF16)
                    scatter_copy(c, b + 1).start()
                else:
                    psum[seg(low), cuts[c]] = term.astype(BF16)
            across_copy(c).start()
            spread(c)

        def part_copy(c, d):
            return remote(ubuf.at[i, :, ucuts[c]], ubuf.at[i, :, ucuts[c]], u_ss.at[0], u_rs.at[c], {"mp": lax.rem(i + d, n_mp)})

        def part_wait(c, count):
            came = ubuf.at[pl.ds(0, count), :, ucuts[c]]
            remote(came, came, u_ss.at[0], u_rs.at[c], {"cand": j}).wait_recv()

        with scope("firstpart"):
            @pl.when(pool_side)
            def _():
                build_onehot()
                pool_m_copy.wait()
                from_pool(base_mp, pool_m, feat)

        neighbours = (j > 0).astype(jnp.int32) + (j < n_cand - 1).astype(jnp.int32)
        with scope("barrier"):
            pl.semaphore_wait(barrier, jnp.where(user_side, n_cand - 1 + half - 1, neighbours + n_mp - 1))

        with scope("layer1"):
            @pl.when(pool_side)
            def _():
                for d in range(half):
                    pl.semaphore_signal(ready.at[0], inc=1, device_id={"mp": d}, device_id_type=MESH)
                for c in range(n1 + 2):
                    if c < n1:
                        with scope(f"a{c}"):
                            stage_a(c)
                            if low > 0:
                                scatter_copy(c, 0).start()
                        if c == n1 - 1:
                            w2_copy.start()
                    if c >= 2:
                        with scope(f"b{c - 2}"):
                            stage_b(c - 2)

            @pl.when(user_side)
            def _():
                for k in range(1, n_cand):
                    user_copy(k).start()
                with scope("early"):
                    @pl.when(col_pool)
                    def _():
                        build_onehot()
                        pool_c_copy.wait()
                        from_pool(base_col, pool_c, col)

                    @pl.when(jnp.logical_not(col_pool))
                    def _():
                        small_copies[0].wait()

                    for copy in w1_copies:
                        copy.wait()
                    small_copies[2].wait()
                    pl.semaphore_wait(ready.at[0], half)
                with scope("users"):
                    from_all_users()
                rows_of = [user_row(u, i, feat) for u in range(users)]
                if users == 1:
                    lhs[...] = jnp.broadcast_to(rows_of[0], lhs.shape).astype(BF16)
                else:
                    place = lax.broadcasted_iota(jnp.int32, lhs.shape, 0)
                    filled = jnp.zeros(lhs.shape, F32)
                    for u in range(users):
                        filled = jnp.where(place == u, rows_of[u], filled)
                    lhs[...] = filled.astype(BF16)
                for c, cut in enumerate(ucuts):
                    with scope(f"um{c}"):
                        term = jnp.dot(lhs[...], w1_v[:, cut], preferred_element_type=F32)
                        ubuf[i, :, cut] = term[0:users]
                        for d in range(n_mp - 1, 0, -1):
                            part_copy(c, d).start()
                    if c == 0:
                        @pl.when(jnp.logical_not(col_pool))
                        def _():
                            for u in range(users):
                                ucol[u : u + 1, :] = user_row(u, j, col).astype(BF16)
                            ucol_copy().start()

        def take_across(c):
            @pl.when(user_side)
            def _():
                with scope(f"across{c}"):
                    across_copy(c).wait_recv()
                spread(c)

        ahead = min(2, n1)
        with scope("bases"):
            w3_copy.start()

            for c in range(ahead):
                take_across(c)

            @pl.when(user_side)
            def _():
                from_user(base_mp, i, feat)

            @pl.when(jnp.logical_and(col_pool, pool_side))
            def _():
                pool_c_copy.wait()
                from_pool(base_col, pool_c, col)

            @pl.when(jnp.logical_not(col_pool))
            def _():
                @pl.when(pool_side)
                def _():
                    ucol_copy().wait_recv()

                for p in range(n_mp):
                    u = user_of(p)
                    value = ucol[u : u + 1, :].astype(F32)
                    base_col[p * block : (p + 1) * block, :] = jnp.broadcast_to(value, (block, col)).astype(BF16)

            for copy in small_copies[3:]:
                copy.wait()

            @pl.when(pool_side)
            def _():
                for copy in small_copies[1:3]:
                    copy.wait()

        def first_cross(c):
            with scope(f"gw{c}"):
                for b in range(low - 1, -1, -1):
                    gather_wait(c, b)
                    if b > 0:
                        gather_copy(c, b - 1).start()
            for u, ucut in enumerate(ucuts):
                if ucut.start != cuts[c].start:
                    continue
                with scope(f"pw{u}"):
                    @pl.when(user_side)
                    def _():
                        if half > 1:
                            part_wait(u, half - 1)

                    @pl.when(pool_side)
                    def _():
                        part_wait(u, half)

            cols = cuts[c]
            added = b1_ref[:, cols]
            for src in range(half):
                added = added + ubuf[src, :, cols]
            for p in range(n_mp):
                r = slice(p * block, (p + 1) * block)
                u = user_of(p)
                base = base_col[r, cols].astype(F32)
                cross1[r, cols] = (base * (psum[r, cols].astype(F32) + added[u : u + 1]) + base).astype(BF16)

        halves = [slice(g * part, (g + 1) * part) for g in range(2)]
        toward = 1 - 2 * nd

        def z_copy(g, n, way, src, step):
            at = (halves[g], zcuts[g][n])
            return remote(
                src.at[at], zr.at[(way,) + at], z_ss.at[way], z_rs.at[way, g, n], {"cand": j + step}
            )

        def z_wait(g, n, way):
            at = (halves[g], zcuts[g][n])
            remote(q_send.at[at], zr.at[(way,) + at], z_ss.at[way], z_rs.at[way, g, n], {"cand": j}).wait_recv()

        def first_out(cols):
            last = cuts[n1 - 1]
            term = jnp.dot(cross1[:, last], w2_v[last, cols], preferred_element_type=F32)
            if n1 > 1:
                term = acc2[:, cols] + term
            owner = (j == i * ratio + cols.start // col).astype(F32)
            inside = cols.start % col
            carried = cross1[:, inside : inside + cols.stop - cols.start].astype(F32)
            term = base_mp[:, cols].astype(F32) * (term + owner * b2_ref[:, cols]) + owner * carried
            q_send[:, cols] = term.astype(BF16)

        for c in range(n1):
            first_cross(c)
            if c + ahead < n1:
                take_across(c + ahead)
            if c == 0:
                w2_copy.wait()
            if c < n1 - 1:
                with scope(f"l2_{c}"):
                    term = jnp.dot(cross1[:, cuts[c]], w2_v[cuts[c], :], preferred_element_type=F32)
                    acc2[...] = term if c == 0 else acc2[...] + term
        for s in range(0, len(zcuts[0]), 2):
            with scope(f"q{s}"):
                for cols in zcuts[0][s : s + 2]:
                    first_out(cols)

                @pl.when(end)
                def _():
                    for n in range(s, min(s + 2, len(zcuts[0]))):
                        z_copy(0, n, nd, q_send, toward).start()

        @pl.when(end)
        def _():
            for g in range(1, len(zcuts)):
                for n in range(len(zcuts[g])):
                    z_copy(g, n, nd, q_send, toward).start()

        def pass_on(g, n, way, step):
            at = (halves[g], zcuts[g][n])
            zs[(way,) + at] = (zr[(way,) + at].astype(F32) + q_send[at].astype(F32)).astype(BF16)
            z_copy(g, n, way, zs.at[way], step).start()

        def near(g, n):
            @pl.when(inner)
            def _():
                with scope(f"near{g}_{n}"):
                    z_wait(g, n, nd)
                pass_on(g, n, nd, toward)

        def far(g, n):
            with scope(f"far{g}_{n}"):
                z_wait(g, n, 1 - nd)

            @pl.when(inner)
            def _():
                pass_on(g, n, 1 - nd, -toward)

        def third(g, n):
            cols = zcuts[g][n]
            r = halves[g]
            value = (
                q_send[r, cols].astype(F32) + zr[0, r, cols].astype(F32) + zr[1, r, cols].astype(F32)
            ).astype(BF16)
            x3[r, cols] = value
            if g == 0 and n == 0:
                w3_copy.wait()
            term = jnp.dot(value, w3_v[cols, :], preferred_element_type=F32)
            acc3[r, :] = term if n == 0 else acc3[r, :] + term

        side = i // half

        def last_copy(c, peer):
            r = pl.ds(pl.multiple_of(peer * block, block), block)
            cols = slice(c * cw3, (c + 1) * cw3)
            return remote(send3.at[r, cols], recv3.at[i, :, cols], c_ss.at[0], c_rs.at[c], {"mp": peer})

        owner3 = (i == j // ratio).astype(F32)

        def q_copy(g, di, dj):
            return remote(
                q_mine.at[g], q_all.at[me], q_sem.at[0], q_sem.at[1],
                {"mp": g * half + lax.rem(i + di, half), "cand": lax.rem(j + dj, n_cand)},
            )

        def send_scores(g):
            q_mine[g] = jnp.sum(q_rows[...].T, axis=0, keepdims=True)
            same = side == g

            @pl.when(same)
            def _():
                q_all[me] = q_mine[g]

            def each(dj, carry):
                for di in range(half):
                    q_copy(g, di, dj).start()
                return carry

            far_first = [n_cand // 2] + [d for k in range(1, (n_cand + 1) // 2) for d in (n_cand // 2 - k, n_cand // 2 + k)]
            if n_cand <= 4:
                for dj in far_first:
                    if dj:
                        each(dj, 0)
            else:
                lax.fori_loop(1, n_cand, each, 0)
            for di in range(1, half):
                q_copy(g, di, 0).start()

            @pl.when(jnp.logical_not(same))
            def _():
                q_copy(g, 0, 0).start()

        def epilogue(g):
            r = halves[g]
            same = side == g
            for c in range(n3):
                cols = slice(c * cw3, (c + 1) * cw3)
                if ratio == 1:
                    carried = x3[r, cols]
                else:
                    carried = x3[r, pl.ds(pl.multiple_of(lax.rem(j, ratio) * col + c * cw3, 128), cw3)]
                term = (
                    base_col[r, cols].astype(F32) * (acc3[r, cols] + owner3 * b3_ref[:, cols])
                    + owner3 * carried.astype(F32)
                )
                acc3[r, cols] = term
                send3[r, cols] = term.astype(BF16)

                for d in range(1, half):
                    last_copy(c, g * half + lax.rem(i + d, half)).start()

                @pl.when(jnp.logical_not(same))
                def _():
                    last_copy(c, g * half + lax.rem(i, half)).start()

            lanes = jnp.zeros((part, 128), F32)
            for k in range(0, col, 128):
                lanes = lanes + acc3[r, k : k + 128] * score_ref[k : k + 128].astype(F32).reshape(1, 128)
            q_rows[0:part, :] = lanes
            send_scores(g)

        events = [(g, n) for g in range(2) for n in range(len(zcuts[g]))]
        if q_width > part:
            q_rows[part:, :] = jnp.zeros((q_width - part, 128), F32)

        def stream(skew):
            first_done = max(len(zcuts[0]) - 1, len(events) - skew)
            for s in range(len(events) + skew):
                if s < len(events):
                    near(*events[s])
                if s < skew:
                    continue
                g, n = events[s - skew]
                far(g, n)
                with scope(f"third{g}_{n}"):
                    third(g, n)
                if s - skew == first_done:
                    with scope("epi0"):
                        epilogue(0)
            with scope("epi1"):
                epilogue(1)

        @pl.when(nd == 0)
        def _():
            stream(min(13, len(events)))

        @pl.when(nd == 1)
        def _():
            stream(min(5, len(events)))

        mine = pl.ds(pl.multiple_of(i * block, block), block)
        for c in range(n3):
            cols = slice(c * cw3, (c + 1) * cw3)
            with scope(f"last{c}"):
                came = recv3.at[pl.ds(0, n_mp - 1), :, cols]
                remote(came, came, c_ss.at[0], c_rs.at[c], {"mp": i}).wait_recv()
            term = acc3[mine, cols]
            for d in range(1, n_mp):
                term = term + recv3[lax.rem(i - d + n_mp, n_mp), :, cols].astype(F32)
            out_ref[:, cols] = term.astype(BF16)

        with scope("qwait"):
            rest = q_all.at[pl.ds(0, group - 1)]
            remote(rest, rest, q_sem.at[0], q_sem.at[1], {"cand": j}).wait_recv()
            total = jnp.sum(q_all[...], axis=0)
            for k in range(n_mp):
                p = k % half

                @pl.when(i == k)
                def _():
                    logit_ref[...] = total[:, p * block : (p + 1) * block]

        def sent(ref, sem):
            remote(ref, ref, sem, sem, {"cand": j}).wait_send()

        with scope("sent"):
            @pl.when(pool_side)
            def _():
                for b in range(low):
                    sent(recv1.at[b, pl.ds(0, rows >> (b + 1)), :], a_ss.at[b])
                sent(psum.at[seg(low), :], x_ss.at[0])

            @pl.when(user_side)
            def _():
                sent(others, user_sem.at[0])

                @pl.when(jnp.logical_not(col_pool))
                def _():
                    sent(ucol, ucol_sem.at[0])

                sent(ubuf.at[pl.ds(0, n_mp - 1)], u_ss.at[0])

            for b in range(low):
                sent(psum.at[seg(b + 1), :], g_ss.at[b])
            sent(q_send, z_ss.at[nd])

            @pl.when(inner)
            def _():
                sent(q_send, z_ss.at[1 - nd])

            sent(recv3.at[pl.ds(0, n_mp - 1)], c_ss.at[0])
            sent(rest, q_sem.at[0])

    return kernel


def solution(mesh):
    n_mp, n_cand = mesh.shape["mp"], mesh.shape["cand"]

    def body(
        user_feats, user_slot, cand_pool, cand_ids, first_weight, first_bias,
        second_weight, second_bias, third_weight, third_bias, score_weight,
    ):
        slots_each, half_width = user_feats.shape
        users, per_user = cand_ids.shape
        rows = users * per_user
        pool_count = cand_pool.shape[0]
        feat, col = first_weight.shape
        wide = min(512, col)
        ucuts = [slice(k, k + wide) for k in range(0, col, wide)]
        cuts = list(ucuts)
        step = min(256, col, feat)
        zcuts = [[slice(k, k + step) for k in range(0, feat, step)] for _ in range(2)]
        if step > 128:
            zcuts[1][-1:] = [slice(feat - step, feat - step // 2), slice(feat - step // 2, feat)]
        n1, n2 = len(cuts), len(zcuts[1])
        n3 = max(1, col // 512)
        lhs_rows = -(-users // 16) * 16
        bits = n_mp.bit_length() - 1
        low = max(1, bits - 1)
        half = n_mp // 2
        block = rows // n_mp
        group = n_mp * n_cand
        shapes = (rows, per_user, users, slots_each, half_width, pool_count, feat, col, cuts, ucuts, zcuts, n3)
        vmem = pl.BlockSpec(memory_space=pltpu.VMEM)
        hbm = pl.BlockSpec(memory_space=pl.ANY)
        dma = pltpu.SemaphoreType.DMA
        crossed, logits = pl.pallas_call(
            make_kernel(n_mp, n_cand, shapes),
            out_shape=(
                pltpu.VMEM((block, col), BF16),
                pltpu.VMEM((1, block), F32),
            ),
            in_specs=[hbm] * 11,
            out_specs=(vmem, vmem),
            scratch_shapes=[
                pltpu.SMEM((1, users), jnp.int32),
                pltpu.VMEM((users, per_user), jnp.int32),
                pltpu.VMEM((1, col), F32),
                pltpu.VMEM((1, feat), F32),
                pltpu.VMEM((1, col), F32),
                pltpu.VMEM((col,), BF16),
                dma((7,)),
                pltpu.VMEM((n_cand, slots_each, half_width), BF16),
                pltpu.VMEM((users, col), BF16),
                pltpu.VMEM((pool_count, feat), BF16),
                pltpu.VMEM((pool_count, col), BF16),
                pltpu.VMEM((feat, col), BF16),
                pltpu.VMEM((col, feat), BF16),
                pltpu.VMEM((feat, col), BF16),
                pltpu.VMEM((rows, pool_count), BF16),
                pltpu.VMEM((rows, feat), BF16),
                pltpu.VMEM((rows, col), BF16),
                pltpu.VMEM((lhs_rows, feat), BF16),
                pltpu.VMEM((rows, col), F32),
                pltpu.VMEM((rows, col), BF16),
                pltpu.VMEM((low, rows // 2, col), BF16),
                pltpu.VMEM((rows, col), BF16),
                pltpu.VMEM((n_mp, users, col), F32),
                pltpu.VMEM((rows, col), BF16),
                pltpu.VMEM((rows, feat), F32),
                pltpu.VMEM((rows, feat), BF16),
                pltpu.VMEM((2, rows, feat), BF16),
                pltpu.VMEM((2, rows, feat), BF16),
                pltpu.VMEM((rows, feat), BF16),
                pltpu.VMEM((rows, col), F32),
                pltpu.VMEM((rows, col), BF16),
                pltpu.VMEM((n_mp, block, col), BF16),
                pltpu.VMEM((max(rows // 2, 128), 128), F32),
                pltpu.VMEM((2, 1, max(rows // 2, 128)), F32),
                pltpu.VMEM((group, 1, max(rows // 2, 128)), F32),
                dma((4 + n1,)),
                dma((2,)),
                dma((2,)),
                pltpu.SemaphoreType.REGULAR((1,)),
                dma((low,)),
                dma((low, n1)),
                dma((1,)),
                dma((n1,)),
                dma((low,)),
                dma((low, n1)),
                dma((1,)),
                dma((len(ucuts),)),
                dma((2,)),
                dma((2, 2, n2)),
                dma((1,)),
                dma((n3,)),
                dma((2,)),
            ],
            compiler_params=pltpu.CompilerParams(
                collective_id=0, has_side_effects=True, vmem_limit_bytes=67043328 - 3000 * 1024
            ),
        )(
            user_feats, user_slot.reshape(1, -1), cand_pool, cand_ids, first_weight, first_bias.reshape(1, -1),
            second_weight, second_bias.reshape(1, -1), third_weight, third_bias.reshape(1, -1),
            score_weight,
        )
        crossed, logits = pl.pallas_call(
            hand_on,
            out_shape=(
                jax.ShapeDtypeStruct((block, col), BF16),
                jax.ShapeDtypeStruct((1, block), F32),
            ),
            in_specs=[vmem, vmem],
            out_specs=(hbm, hbm),
            scratch_shapes=[dma((2,))],
            compiler_params=pltpu.CompilerParams(vmem_limit_bytes=1024 * 1024),
        )(crossed, logits)
        return crossed, logits.reshape(-1)

    in_specs = (
        P(("groups", "cand"), None),
        P("groups"),
        P("groups", None),
        P("groups", None),
        P("mp", "cand"),
        P("cand"),
        P("cand", "mp"),
        P("mp"),
        P("mp", "cand"),
        P("cand"),
        P("cand"),
    )
    out_specs = (P(("groups", "mp"), "cand"), P(("groups", "mp")))
    return jax.shard_map(body, mesh=mesh, in_specs=in_specs, out_specs=out_specs, check_vma=False)
```

time: 34.6 us -> 32.5 us (0.939)
  Pallas kernels: 33.2 us -> 31.1 us
    pallas_call x1, Pallas kernels: 32.5 us -> 30.4 us  [body(): pl.pallas_call(make_kernel(n_mp, n_cand, shapes), out_shape=(pltpu.VMEM((...]
where the time goes in v3:
time: 32.5 us; the launch traced here: 32.4 us
  Pallas kernels  31.1 us (96%)
  between operations  1.29 us (4%)
    pallas_call x1, Pallas kernels, body(): pl.pallas_call(make_kernel(n_mp, n_cand, shapes), out_shape=(pltpu.VMEM((...  30.4 us
    pallas_call x1, Pallas kernels, body(): pl.pallas_call(hand_on, out_shape=(jax.ShapeDtypeStruct((block, col), BF1...  0.65 us

profile of v3, /device:TPU:0, one launch (start us, length us, event | category | flops | bytes accessed | tf_op | source)
XLA Modules:
  0.0 32.4 jit_solution(13378138795227815695)
XLA Ops:
  1.3 30.4 %shard_map.122 = (bf16[16,2048]{1,0:T(8,128)(2,1)S(1)}, f32[1,16]{1,0:T(1,128)S(1)}) custom-call(bf16[1,4096]{1,0:T(2,128)(2,1)} %user_hbm.1, s32[1,1]{1,0:T(1,128)} %bitcast.5.slot_hbm, bf16[256,4096]{1,0:T(8,128)(2,1)} %pool_hbm.1, s32[1,64]{1,0:T(1,128)} %ids_hbm.1, bf16[2048,2048]{1,0:T(8,128)(2,1)} %w1_hbm.1, f32[1,2048]{1,0:T(1,128)} %bitcast.6, ...), custom_call_target="tpu_custom_call" | custom-call | tf_op jit(solution)/shard_map/pallas_call | solution.py:672
  31.7 0.7 %shard_map.123 = (bf16[16,2048]{1,0:T(8,128)(2,1)}, f32[1,16]{1,0:T(1,128)}) custom-call(bf16[16,2048]{1,0:T(8,128)(2,1)S(1)} %get-tuple-element.6.crossed_ref, f32[1,16]{1,0:T(1,128)S(1)} %get-tuple-element.7.logit_ref), custom_call_target="tpu_custom_call" | custom-call | tf_op jit(solution)/shard_map/pallas_call | solution.py:742

commit v4 on v3

--- a/solution.py
+++ b/solution.py
@@ -28,7 +28,7 @@
 
 
 def make_kernel(n_mp, n_cand, shapes):
-    rows, per_user, users, slots_each, half_width, pool_count, feat, col, cuts, ucuts, zcuts, n3 = shapes
+    rows, per_user, users, slots_each, half_width, pool_count, feat, col, cuts, ucuts, zcuts, spans, n3 = shapes
     cw3 = col // n3
     n1 = len(cuts)
     bits = n_mp.bit_length() - 1
@@ -37,8 +37,10 @@
     block = rows // n_mp
     ratio = feat // col
     group = n_mp * n_cand
-    part = rows // 2
-    q_width = max(part, 128)
+    halves = [slice(lo * block, hi * block) for lo, hi in spans]
+    events = [(g, n) for g in range(len(spans)) for n in range(len(zcuts[g]))]
+    place = {event: k for k, event in enumerate(events)}
+    q_width = max([128] + [r.stop - r.start for r in halves])
     first_pool_col = half_width // col
 
     def user_of(p):
@@ -47,16 +49,18 @@
     def kernel(
         user_hbm, slot_hbm, pool_hbm, ids_hbm, w1_hbm, b1_hbm, w2_hbm, b2_hbm, w3_hbm, b3_hbm, score_hbm,
         out_ref, logit_ref,
-        slot_ref, ids_ref, b1_ref, b2_ref, b3_ref, score_ref, small_sem, slots, ucol, pool_m, pool_c, w1_v, w2_v, w3_v,
-        onehot, base_mp, base_col, lhs, acc1, send1, recv1, psum, ubuf, cross1, acc2, q_send, zr, zs, x3, acc3, send3, recv3,
+        slot_ref, ids_ref, b1_ref, b2_ref, b3_ref, score_ref, small_sem, slots, urow, ucol, pool_m, pool_c, w1_v, w2_v, w3_v,
+        onehot, base_mp, base_col, lhs, acc1, send1, recv1, psum, ubuf, cross1, acc2, q_send, zr, zs, ze, zf, qe, x3, acc3, send3, recv3,
         q_rows, q_mine, q_all,
-        w_sem, user_sem, ucol_sem, ready, a_ss, a_rs, x_ss, x_rs, g_ss, g_rs, u_ss, u_rs, z_ss, z_rs, c_ss, c_rs, q_sem,
+        w_sem, user_sem, urow_ss, urow_rs, ucol_sem, ready, a_ss, a_rs, x_ss, x_rs, g_ss, g_rs, u_ss, u_rs, z_ss, z_rs, ze_rs, qe_ss, qe_rs, ef_ss, c_ss, c_rs, q_sem,
     ):
         i = lax.axis_index("mp")
         j = lax.axis_index("cand")
         me = i * n_cand + j
         user_side = i < half
         pool_side = jnp.logical_not(user_side)
+        leader = i == half - 1
+        follower = jnp.logical_not(leader)
 
         def remote(src, dst, ss, rs, where):
             return pltpu.make_async_remote_copy(
@@ -69,9 +73,20 @@
                 pl.semaphore_signal(barrier, inc=1, device_id={"cand": lax.rem(j + d, n_cand)}, device_id_type=MESH)
                 return carry
 
+            @pl.when(leader)
+            def _():
+                lax.fori_loop(1, n_cand, greet, 0, unroll=n_cand <= 4)
+
+            @pl.when(jnp.logical_and(follower, j > 0))
+            def _():
+                pl.semaphore_signal(barrier, inc=1, device_id={"cand": j - 1}, device_id_type=MESH)
+
+            @pl.when(jnp.logical_and(follower, j < n_cand - 1))
+            def _():
+                pl.semaphore_signal(barrier, inc=1, device_id={"cand": j + 1}, device_id_type=MESH)
+
             @pl.when(user_side)
             def _():
-                lax.fori_loop(1, n_cand, greet, 0, unroll=n_cand <= 4)
                 for d in range(1, n_mp):
                     pl.semaphore_signal(barrier, inc=1, device_id={"mp": lax.rem(i + d, n_mp)}, device_id_type=MESH)
 
@@ -81,14 +96,6 @@
                     pl.semaphore_signal(
                         barrier, inc=1, device_id={"mp": half + lax.rem(i + d, half)}, device_id_type=MESH
                     )
-
-                @pl.when(j > 0)
-                def _():
-                    pl.semaphore_signal(barrier, inc=1, device_id={"cand": j - 1}, device_id_type=MESH)
-
-                @pl.when(j < n_cand - 1)
-                def _():
-                    pl.semaphore_signal(barrier, inc=1, device_id={"cand": j + 1}, device_id_type=MESH)
 
         small_copies = [
             pltpu.make_async_copy(src, dst, small_sem.at[k])
@@ -155,19 +162,22 @@
             for c in range(0, width, 256):
                 dst[:, c : c + 256] = jnp.dot(onehot[...], src[:, c : c + 256], preferred_element_type=F32).astype(BF16)
 
-        def user_row(u, index, width):
-            start = pl.multiple_of(index * width, 128)
+        def user_row(u):
             slot = slot_ref[0, u]
-            row = slots[slot // slots_each, :, pl.ds(start, width)].astype(F32)
+            row = slots[slot // slots_each].astype(F32)
             if slots_each > 1:
                 pick = lax.broadcasted_iota(jnp.int32, row.shape, 0) == lax.rem(slot, slots_each)
                 row = jnp.sum(jnp.where(pick, row, 0.0), axis=0, keepdims=True)
             return row
 
         def from_user(dst, index, width):
-            rows_of = [user_row(u, index, width) for u in range(users)]
+            row = urow[:, pl.ds(pl.multiple_of(index * width, 128), width)].astype(F32)
             for p in range(n_mp):
-                dst[p * block : (p + 1) * block, :] = jnp.broadcast_to(rows_of[user_of(p)], (block, width)).astype(BF16)
+                u = user_of(p)
+                dst[p * block : (p + 1) * block, :] = jnp.broadcast_to(row[u : u + 1], (block, width)).astype(BF16)
+
+        def urow_copy(d):
+            return remote(urow, urow, urow_ss.at[d], urow_rs.at[0], {"mp": lax.rem(i + d, half)})
 
         def user_copy(k):
             d = jnp.where(j < n_cand // 2, n_cand - k, k)
@@ -267,29 +277,44 @@
 
         neighbours = (j > 0).astype(jnp.int32) + (j < n_cand - 1).astype(jnp.int32)
         with scope("barrier"):
-            pl.semaphore_wait(barrier, jnp.where(user_side, n_cand - 1 + half - 1, neighbours + n_mp - 1))
+            pl.semaphore_wait(
+                barrier,
+                jnp.where(leader, n_cand - 1, neighbours) + jnp.where(user_side, half - 1, n_mp - 1),
+            )
 
         with scope("layer1"):
             @pl.when(pool_side)
             def _():
                 for d in range(half):
                     pl.semaphore_signal(ready.at[0], inc=1, device_id={"mp": d}, device_id_type=MESH)
-                for c in range(n1 + 2):
-                    if c < n1:
-                        with scope(f"a{c}"):
-                            stage_a(c)
-                            if low > 0:
-                                scatter_copy(c, 0).start()
-                        if c == n1 - 1:
-                            w2_copy.start()
-                    if c >= 2:
-                        with scope(f"b{c - 2}"):
-                            stage_b(c - 2)
+                def pool_part(lag):
+                    for c in range(n1 + lag):
+                        if c < n1:
+                            with scope(f"a{c}"):
+                                stage_a(c)
+                                if low > 0:
+                                    scatter_copy(c, 0).start()
+                            if c == n1 - 1:
+                                w2_copy.start()
+                        if c >= lag:
+                            with scope(f"b{c - lag}"):
+                                stage_b(c - lag)
+
+                @pl.when(bit_of(0) == 0)
+                def _():
+                    pool_part(1)
+
+                @pl.when(bit_of(0) != 0)
+                def _():
+                    pool_part(2)
 
             @pl.when(user_side)
             def _():
-                for k in range(1, n_cand):
-                    user_copy(k).start()
+                @pl.when(leader)
+                def _():
+                    for k in range(1, n_cand):
+                        user_copy(k).start()
+
                 with scope("early"):
                     @pl.when(col_pool)
                     def _():
@@ -306,15 +331,28 @@
                     small_copies[2].wait()
                     pl.semaphore_wait(ready.at[0], half)
                 with scope("users"):
-                    from_all_users()
-                rows_of = [user_row(u, i, feat) for u in range(users)]
+                    @pl.when(leader)
+                    def _():
+                        from_all_users()
+                        for u in range(users):
+                            urow[u : u + 1, :] = user_row(u).astype(BF16)
+                        for d in range(1, half):
+                            urow_copy(d).start()
+
+                    @pl.when(follower)
+                    def _():
+                        if half > 1:
+                            urow_copy(0).wait_recv()
+                        small_copies[1].wait()
+
+                row = urow[:, pl.ds(pl.multiple_of(i * feat, 128), feat)]
                 if users == 1:
-                    lhs[...] = jnp.broadcast_to(rows_of[0], lhs.shape).astype(BF16)
+                    lhs[...] = jnp.broadcast_to(row.astype(F32), lhs.shape).astype(BF16)
                 else:
-                    place = lax.broadcasted_iota(jnp.int32, lhs.shape, 0)
+                    line = lax.broadcasted_iota(jnp.int32, lhs.shape, 0)
                     filled = jnp.zeros(lhs.shape, F32)
                     for u in range(users):
-                        filled = jnp.where(place == u, rows_of[u], filled)
+                        filled = jnp.where(line == u, row[u : u + 1].astype(F32), filled)
                     lhs[...] = filled.astype(BF16)
                 for c, cut in enumerate(ucuts):
                     with scope(f"um{c}"):
@@ -325,8 +363,7 @@
                     if c == 0:
                         @pl.when(jnp.logical_not(col_pool))
                         def _():
-                            for u in range(users):
-                                ucol[u : u + 1, :] = user_row(u, j, col).astype(BF16)
+                            ucol[...] = urow[:, pl.ds(pl.multiple_of(j * col, 128), col)]
                             ucol_copy().start()
 
         def take_across(c):
@@ -400,18 +437,17 @@
                 base = base_col[r, cols].astype(F32)
                 cross1[r, cols] = (base * (psum[r, cols].astype(F32) + added[u : u + 1]) + base).astype(BF16)
 
-        halves = [slice(g * part, (g + 1) * part) for g in range(2)]
         toward = 1 - 2 * nd
 
         def z_copy(g, n, way, src, step):
             at = (halves[g], zcuts[g][n])
             return remote(
-                src.at[at], zr.at[(way,) + at], z_ss.at[way], z_rs.at[way, g, n], {"cand": j + step}
+                src.at[at], zr.at[(way,) + at], z_ss.at[way], z_rs.at[way, place[g, n]], {"cand": j + step}
             )
 
         def z_wait(g, n, way):
             at = (halves[g], zcuts[g][n])
-            remote(q_send.at[at], zr.at[(way,) + at], z_ss.at[way], z_rs.at[way, g, n], {"cand": j}).wait_recv()
+            remote(q_send.at[at], zr.at[(way,) + at], z_ss.at[way], z_rs.at[way, place[g, n]], {"cand": j}).wait_recv()
 
         def first_out(cols):
             last = cuts[n1 - 1]
@@ -434,21 +470,44 @@
                 with scope(f"l2_{c}"):
                     term = jnp.dot(cross1[:, cuts[c]], w2_v[cuts[c], :], preferred_element_type=F32)
                     acc2[...] = term if c == 0 else acc2[...] + term
+        even = bit_of(0) == 0
+        odd = jnp.logical_not(even)
+        detour = jnp.logical_and(even, j == n_cand - 1) if n_cand > 2 else None
+
+        def detour_copy(g, n):
+            at = (halves[g], zcuts[g][n])
+            return remote(
+                q_send.at[at], ze.at[at], z_ss.at[1], ze_rs.at[place[g, n]], {"mp": i + 1, "cand": j - 1}
+            )
+
+        def first_send(g, ns):
+            @pl.when(end if detour is None else jnp.logical_and(end, jnp.logical_not(detour)))
+            def _():
+                for n in ns:
+                    z_copy(g, n, nd, q_send, toward).start()
+
+            if detour is not None:
+                @pl.when(detour)
+                def _():
+                    for n in ns:
+                        detour_copy(g, n).start()
+
+        def lend_copy(s):
+            cols = slice(zcuts[0][s].start, zcuts[0][min(s + 1, len(zcuts[0]) - 1)].stop)
+            return remote(q_send.at[:, cols], qe.at[:, cols], qe_ss.at[0], qe_rs.at[s // 2], {"mp": i + 1 - 2 * bit_of(0)})
+
         for s in range(0, len(zcuts[0]), 2):
             with scope(f"q{s}"):
                 for cols in zcuts[0][s : s + 2]:
                     first_out(cols)
-
-                @pl.when(end)
-                def _():
-                    for n in range(s, min(s + 2, len(zcuts[0]))):
-                        z_copy(0, n, nd, q_send, toward).start()
-
-        @pl.when(end)
-        def _():
-            for g in range(1, len(zcuts)):
-                for n in range(len(zcuts[g])):
-                    z_copy(g, n, nd, q_send, toward).start()
+                first_send(0, range(s, min(s + 2, len(zcuts[0]))))
+
+                @pl.when(jnp.logical_and(inner, even))
+                def _():
+                    lend_copy(s).start()
+
+        for g in range(1, len(zcuts)):
+            first_send(g, range(len(zcuts[g])))
 
         def pass_on(g, n, way, step):
             at = (halves[g], zcuts[g][n])
@@ -456,19 +515,36 @@
             z_copy(g, n, way, zs.at[way], step).start()
 
         def near(g, n):
-            @pl.when(inner)
-            def _():
-                with scope(f"near{g}_{n}"):
-                    z_wait(g, n, nd)
-                pass_on(g, n, nd, toward)
-
-        def far(g, n):
+            with scope(f"near{g}_{n}"):
+                z_wait(g, n, nd)
+            pass_on(g, n, nd, toward)
+
+        def far(g, n, passing):
             with scope(f"far{g}_{n}"):
                 z_wait(g, n, 1 - nd)
-
-            @pl.when(inner)
-            def _():
+            if passing:
                 pass_on(g, n, 1 - nd, -toward)
+
+        def relay(g, n):
+            at = (halves[g], zcuts[g][n])
+            k = place[g, n]
+            with scope(f"relay{g}_{n}"):
+                remote(ze.at[at], ze.at[at], ef_ss.at[0], ze_rs.at[k], {"cand": j}).wait_recv()
+            if g == 0 and n % 2 == 0:
+                lend_copy(n).wait_recv()
+            zf[at] = (ze[at].astype(F32) + qe[at].astype(F32)).astype(BF16)
+
+            @pl.when(j > 1)
+            def _():
+                remote(zf.at[at], ze.at[at], ef_ss.at[0], ze_rs.at[k], {"cand": j - 1}).start()
+
+            @pl.when(j == 1)
+            def _():
+                remote(
+                    zf.at[at], zr.at[(1,) + at], ef_ss.at[0], z_rs.at[1, k], {"mp": i - 1, "cand": j - 1}
+                ).start()
+
+            remote(ze.at[at], zr.at[(1,) + at], ef_ss.at[1], z_rs.at[1, k], {"mp": i - 1}).start()
 
         def third(g, n):
             cols = zcuts[g][n]
@@ -482,8 +558,6 @@
             term = jnp.dot(value, w3_v[cols, :], preferred_element_type=F32)
             acc3[r, :] = term if n == 0 else acc3[r, :] + term
 
-        side = i // half
-
         def last_copy(c, peer):
             r = pl.ds(pl.multiple_of(peer * block, block), block)
             cols = slice(c * cw3, (c + 1) * cw3)
@@ -491,42 +565,23 @@
 
         owner3 = (i == j // ratio).astype(F32)
 
-        def q_copy(g, di, dj):
+        def q_copy(g, peer, dj):
             return remote(
                 q_mine.at[g], q_all.at[me], q_sem.at[0], q_sem.at[1],
-                {"mp": g * half + lax.rem(i + di, half), "cand": lax.rem(j + dj, n_cand)},
+                {"mp": peer, "cand": lax.rem(j + dj, n_cand)},
             )
 
-        def send_scores(g):
-            q_mine[g] = jnp.sum(q_rows[...].T, axis=0, keepdims=True)
-            same = side == g
-
-            @pl.when(same)
-            def _():
-                q_all[me] = q_mine[g]
-
-            def each(dj, carry):
-                for di in range(half):
-                    q_copy(g, di, dj).start()
-                return carry
-
-            far_first = [n_cand // 2] + [d for k in range(1, (n_cand + 1) // 2) for d in (n_cand // 2 - k, n_cand // 2 + k)]
-            if n_cand <= 4:
-                for dj in far_first:
-                    if dj:
-                        each(dj, 0)
-            else:
-                lax.fori_loop(1, n_cand, each, 0)
-            for di in range(1, half):
-                q_copy(g, di, 0).start()
-
-            @pl.when(jnp.logical_not(same))
-            def _():
-                q_copy(g, 0, 0).start()
+        def score_row(lanes, count):
+            if q_width == 128:
+                total = jnp.sum(lanes, axis=1, keepdims=True)
+                row = lax.broadcasted_iota(jnp.int32, lanes.shape, 0)
+                lane = lax.broadcasted_iota(jnp.int32, lanes.shape, 1)
+                return jnp.sum(jnp.where(row == lane, total, 0.0), axis=0, keepdims=True)
+            q_rows[0:count, :] = lanes
+            return jnp.sum(q_rows[...].T, axis=0, keepdims=True)
 
         def epilogue(g):
             r = halves[g]
-            same = side == g
             for c in range(n3):
                 cols = slice(c * cw3, (c + 1) * cw3)
                 if ratio == 1:
@@ -539,48 +594,85 @@
                 )
                 acc3[r, cols] = term
                 send3[r, cols] = term.astype(BF16)
-
-                for d in range(1, half):
-                    last_copy(c, g * half + lax.rem(i + d, half)).start()
-
-                @pl.when(jnp.logical_not(same))
-                def _():
-                    last_copy(c, g * half + lax.rem(i, half)).start()
-
-            lanes = jnp.zeros((part, 128), F32)
+            for peer in range(*spans[g]):
+                @pl.when(i != peer)
+                def _():
+                    for c in range(n3):
+                        last_copy(c, peer).start()
+
+            count = r.stop - r.start
+            lanes = jnp.zeros((count, 128), F32)
             for k in range(0, col, 128):
                 lanes = lanes + acc3[r, k : k + 128] * score_ref[k : k + 128].astype(F32).reshape(1, 128)
-            q_rows[0:part, :] = lanes
-            send_scores(g)
-
-        events = [(g, n) for g in range(2) for n in range(len(zcuts[g]))]
-        if q_width > part:
-            q_rows[part:, :] = jnp.zeros((q_width - part, 128), F32)
-
-        def stream(skew):
-            first_done = max(len(zcuts[0]) - 1, len(events) - skew)
+            q_mine[g] = score_row(lanes, count)
+
+            def each(dj, carry):
+                for peer in range(*spans[g]):
+                    q_copy(g, peer, dj).start()
+                return carry
+
+            if n_cand <= 4:
+                for dj in sorted(range(1, n_cand), key=lambda d: -min(d, n_cand - d)):
+                    each(dj, 0)
+            else:
+                lax.fori_loop(1, n_cand, each, 0)
+            for peer in range(*spans[g]):
+                @pl.when(i != peer)
+                def _():
+                    q_copy(g, peer, 0).start()
+
+                @pl.when(i == peer)
+                def _():
+                    q_all[me] = q_mine[g]
+
+        if q_width > 128:
+            q_rows[...] = jnp.zeros(q_rows.shape, F32)
+
+        def stream(skew, nears, passing, relays):
+            ready_at = len(events) - skew if nears else 0
             for s in range(len(events) + skew):
-                if s < len(events):
+                if nears and s < len(events):
                     near(*events[s])
+                    if relays == 1:
+                        relay(*events[s])
                 if s < skew:
                     continue
                 g, n = events[s - skew]
-                far(g, n)
+                far(g, n, passing)
+                if relays == 2:
+                    relay(g, n)
+                if passing and not nears:
+                    z_wait(g, n, nd)
                 with scope(f"third{g}_{n}"):
                     third(g, n)
-                if s - skew == first_done:
-                    with scope("epi0"):
-                        epilogue(0)
-            with scope("epi1"):
-                epilogue(1)
-
-        @pl.when(nd == 0)
+                for done in range(len(spans)):
+                    last = place[done, len(zcuts[done]) - 1]
+                    if s - skew == max(last, min(ready_at, len(events) - 1)):
+                        with scope(f"epi{done}"):
+                            epilogue(done)
+
+        @pl.when(end)
         def _():
-            stream(min(13, len(events)))
-
-        @pl.when(nd == 1)
-        def _():
-            stream(min(5, len(events)))
+            stream(0, False, False, 0)
+
+        if n_cand > 2:
+            left = nd == 0
+
+            @pl.when(jnp.logical_and(inner, jnp.logical_and(odd, left)))
+            def _():
+                stream(min(11, len(events)), True, True, 2)
+
+            @pl.when(jnp.logical_and(inner, jnp.logical_and(odd, jnp.logical_not(left))))
+            def _():
+                stream(min(2, len(events)), True, True, 1)
+
+            @pl.when(jnp.logical_and(inner, jnp.logical_and(even, left)))
+            def _():
+                stream(min(11, len(events)), True, False, 0)
+
+            @pl.when(jnp.logical_and(inner, jnp.logical_and(even, jnp.logical_not(left))))
+            def _():
+                stream(0, False, True, 0)
 
         mine = pl.ds(pl.multiple_of(i * block, block), block)
         for c in range(n3):
@@ -597,12 +689,11 @@
             rest = q_all.at[pl.ds(0, group - 1)]
             remote(rest, rest, q_sem.at[0], q_sem.at[1], {"cand": j}).wait_recv()
             total = jnp.sum(q_all[...], axis=0)
-            for k in range(n_mp):
-                p = k % half
-
-                @pl.when(i == k)
-                def _():
-                    logit_ref[...] = total[:, p * block : (p + 1) * block]
+            for lo, hi in spans:
+                for k in range(lo, hi):
+                    @pl.when(i == k)
+                    def _():
+                        logit_ref[...] = total[:, (k - lo) * block : (k - lo + 1) * block]
 
         def sent(ref, sem):
             remote(ref, ref, sem, sem, {"cand": j}).wait_send()
@@ -616,7 +707,11 @@
 
             @pl.when(user_side)
             def _():
-                sent(others, user_sem.at[0])
+                @pl.when(leader)
+                def _():
+                    sent(others, user_sem.at[0])
+                    for d in range(1, half):
+                        sent(urow, urow_ss.at[d])
 
                 @pl.when(jnp.logical_not(col_pool))
                 def _():
@@ -626,11 +721,22 @@
 
             for b in range(low):
                 sent(psum.at[seg(b + 1), :], g_ss.at[b])
-            sent(q_send, z_ss.at[nd])
+            @pl.when(end)
+            def _():
+                sent(q_send, z_ss.at[nd])
 
             @pl.when(inner)
             def _():
-                sent(q_send, z_ss.at[1 - nd])
+                sent(q_send, z_ss.at[0])
+
+            @pl.when(jnp.logical_and(inner, odd))
+            def _():
+                for sem in (z_ss.at[1], ef_ss.at[0], ef_ss.at[1]):
+                    sent(q_send, sem)
+
+            @pl.when(jnp.logical_and(inner, even))
+            def _():
+                sent(q_send, qe_ss.at[0])
 
             sent(recv3.at[pl.ds(0, n_mp - 1)], c_ss.at[0])
             sent(rest, q_sem.at[0])
@@ -653,19 +759,24 @@
         wide = min(512, col)
         ucuts = [slice(k, k + wide) for k in range(0, col, wide)]
         cuts = list(ucuts)
-        step = min(256, col, feat)
-        zcuts = [[slice(k, k + step) for k in range(0, feat, step)] for _ in range(2)]
+        half = n_mp // 2
+        spans = [(0, half), (half, n_mp)]
+        if half > 1:
+            spans[1:] = [(half, half + half // 2), (half + half // 2, n_mp)]
+        zcuts = []
+        for lo, hi in spans:
+            step = min(256 * half // (hi - lo), col, feat)
+            zcuts.append([slice(k, k + step) for k in range(0, feat, step)])
         if step > 128:
-            zcuts[1][-1:] = [slice(feat - step, feat - step // 2), slice(feat - step // 2, feat)]
-        n1, n2 = len(cuts), len(zcuts[1])
+            zcuts[-1][-1:] = [slice(feat - step, feat - step // 2), slice(feat - step // 2, feat)]
+        n1 = len(cuts)
         n3 = max(1, col // 512)
         lhs_rows = -(-users // 16) * 16
         bits = n_mp.bit_length() - 1
         low = max(1, bits - 1)
-        half = n_mp // 2
         block = rows // n_mp
         group = n_mp * n_cand
-        shapes = (rows, per_user, users, slots_each, half_width, pool_count, feat, col, cuts, ucuts, zcuts, n3)
+        shapes = (rows, per_user, users, slots_each, half_width, pool_count, feat, col, cuts, ucuts, zcuts, spans, n3)
         vmem = pl.BlockSpec(memory_space=pltpu.VMEM)
         hbm = pl.BlockSpec(memory_space=pl.ANY)
         dma = pltpu.SemaphoreType.DMA
@@ -686,6 +797,7 @@
                 pltpu.VMEM((col,), BF16),
                 dma((7,)),
                 pltpu.VMEM((n_cand, slots_each, half_width), BF16),
+                pltpu.VMEM((users, half_width), BF16),
                 pltpu.VMEM((users, col), BF16),
                 pltpu.VMEM((pool_count, feat), BF16),
                 pltpu.VMEM((pool_count, col), BF16),
@@ -707,14 +819,19 @@
                 pltpu.VMEM((2, rows, feat), BF16),
                 pltpu.VMEM((2, rows, feat), BF16),
                 pltpu.VMEM((rows, feat), BF16),
+                pltpu.VMEM((rows, feat), BF16),
+                pltpu.VMEM((rows, feat), BF16),
+                pltpu.VMEM((rows, feat), BF16),
                 pltpu.VMEM((rows, col), F32),
                 pltpu.VMEM((rows, col), BF16),
                 pltpu.VMEM((n_mp, block, col), BF16),
                 pltpu.VMEM((max(rows // 2, 128), 128), F32),
-                pltpu.VMEM((2, 1, max(rows // 2, 128)), F32),
+                pltpu.VMEM((len(spans), 1, max(rows // 2, 128)), F32),
                 pltpu.VMEM((group, 1, max(rows // 2, 128)), F32),
                 dma((4 + n1,)),
                 dma((2,)),
+                dma((half,)),
+                dma((1,)),
                 dma((2,)),
                 pltpu.SemaphoreType.REGULAR((1,)),
                 dma((low,)),
@@ -726,7 +843,11 @@
                 dma((1,)),
                 dma((len(ucuts),)),
                 dma((2,)),
-                dma((2, 2, n2)),
+                dma((2, sum(len(part) for part in zcuts))),
+                dma((sum(len(part) for part in zcuts),)),
+                dma((1,)),
+                dma((-(-len(zcuts[0]) // 2),)),
+                dma((2,)),
                 dma((1,)),
                 dma((n3,)),
                 dma((2,)),

time: 32.5 us -> 31.2 us (0.960)
  Pallas kernels: 31.1 us -> 29.6 us
    pallas_call x1, Pallas kernels: 30.4 us -> 28.9 us  [body(): pl.pallas_call(make_kernel(n_mp, n_cand, shapes), out_shape=(pltpu.VMEM((...]
where the time goes in v4:
time: 31.2 us; the launch traced here: 31 us
  Pallas kernels  29.6 us (95%)
  between operations  1.45 us (5%)
    pallas_call x1, Pallas kernels, body(): pl.pallas_call(make_kernel(n_mp, n_cand, shapes), out_shape=(pltpu.VMEM((...  28.9 us
    pallas_call x1, Pallas kernels, body(): pl.pallas_call(hand_on, out_shape=(jax.ShapeDtypeStruct((block, col), BF1...  0.65 us

profile of v4, /device:TPU:0, one launch (start us, length us, event | category | flops | bytes accessed | tf_op | source)
XLA Modules:
  0.0 31.0 jit_solution(10859593396669849749)
XLA Ops:
  1.3 28.9 %shard_map.122 = (bf16[16,2048]{1,0:T(8,128)(2,1)S(1)}, f32[1,16]{1,0:T(1,128)S(1)}) custom-call(bf16[1,4096]{1,0:T(2,128)(2,1)} %user_hbm.1, s32[1,1]{1,0:T(1,128)} %bitcast.5.slot_hbm, bf16[256,4096]{1,0:T(8,128)(2,1)} %pool_hbm.1, s32[1,64]{1,0:T(1,128)} %ids_hbm.1, bf16[2048,2048]{1,0:T(8,128)(2,1)} %w1_hbm.1, f32[1,2048]{1,0:T(1,128)} %bitcast.6, ...), custom_call_target="tpu_custom_call" | custom-call | tf_op jit(solution)/shard_map/pallas_call | solution.py:783
  30.2 0.7 %shard_map.123 = (bf16[16,2048]{1,0:T(8,128)(2,1)}, f32[1,16]{1,0:T(1,128)}) custom-call(bf16[16,2048]{1,0:T(8,128)(2,1)S(1)} %get-tuple-element.6.crossed_ref, f32[1,16]{1,0:T(1,128)S(1)} %get-tuple-element.7.logit_ref), custom_call_target="tpu_custom_call" | custom-call | tf_op jit(solution)/shard_map/pallas_call | solution.py:863

commit v5 on v4

--- a/solution.py
+++ b/solution.py
@@ -198,68 +198,65 @@
         def partner(b):
             return i + (1 << b) * (1 - 2 * bit_of(b))
 
-        lows = [0]
-        for b in range(bits):
-            lows.append(lows[b] + bit_of(b) * (rows >> (b + 1)))
-
-        def seg(b):
-            size = rows >> b
-            if b == 0:
-                return pl.ds(0, rows)
-            return pl.ds(pl.multiple_of(lows[b], size), size)
-
-        def other(b):
-            size = rows >> (b + 1)
-            start = lows[b] + (1 - bit_of(b)) * size
-            return pl.ds(pl.multiple_of(start, size), size)
-
-        def scatter_copy(c, b):
-            size = rows >> (b + 1)
+        def ones(b):
+            return lax.rem(i, 1 << b) == (1 << b) - 1
+
+        root = ones(low)
+        leaf = jnp.logical_not(root)
+
+        def tree_copy(c, b):
             return remote(
-                send1.at[other(b), cuts[c]], recv1.at[b, pl.ds(0, size), cuts[c]], a_ss.at[b], a_rs.at[b, c], {"mp": partner(b)}
+                send1.at[:, cuts[c]], recv1.at[b, :, cuts[c]], a_ss.at[b], a_rs.at[b, c], {"mp": partner(b)}
             )
 
         def across_copy(c):
             return remote(
-                psum.at[seg(low), cuts[c]], psum.at[seg(low), cuts[c]], x_ss.at[0], x_rs.at[c], {"mp": lax.rem(i + half, n_mp)}
+                psum.at[:, cuts[c]], psum.at[:, cuts[c]], x_ss.at[0], x_rs.at[c], {"mp": lax.rem(i + half, n_mp)}
             )
 
-        def gather_copy(c, b):
-            return remote(
-                psum.at[seg(b + 1), cuts[c]], psum.at[seg(b + 1), cuts[c]], g_ss.at[b], g_rs.at[b, c], {"mp": partner(b)}
-            )
-
-        def gather_wait(c, b):
-            remote(
-                psum.at[other(b), cuts[c]], psum.at[other(b), cuts[c]], g_ss.at[b], g_rs.at[b, c], {"mp": partner(b)}
-            ).wait_recv()
-
-        def spread(c):
-            if low > 0:
-                gather_copy(c, low - 1).start()
-
-        def stage_a(c):
+        def spread_copy(c, b):
+            return remote(psum.at[:, cuts[c]], psum.at[:, cuts[c]], g_ss.at[b], g_rs.at[c], {"mp": partner(b)})
+
+        def reduce(c, b):
+            cut = cuts[c]
+            if b == low:
+                psum[:, cut] = acc1[:, cut].astype(BF16)
+                hand_out(c)
+                return
+
+            @pl.when(bit_of(b) == 0)
+            def _():
+                send1[:, cut] = acc1[:, cut].astype(BF16)
+                tree_copy(c, b).start()
+
+            @pl.when(bit_of(b) != 0)
+            def _():
+                tree_copy(c, b).wait_recv()
+                acc1[:, cut] = acc1[:, cut] + recv1[b, :, cut].astype(F32)
+                reduce(c, b + 1)
+
+        def hand_out(c):
+            across_copy(c).start()
+            for b in range(low - 1, -1, -1):
+                spread_copy(c, b).start()
+
+        def stage_a(c, sends):
             w1_copies[c].wait()
             term = jnp.dot(base_mp[...], w1_v[:, cuts[c]], preferred_element_type=F32)
-            if low > 0:
+            if sends:
+                send1[:, cuts[c]] = term.astype(BF16)
+                tree_copy(c, 0).start()
+            else:
                 acc1[:, cuts[c]] = term
-                send1[:, cuts[c]] = term.astype(BF16)
+
+        def stage_b(c):
+            if low == 1:
+                cut = cuts[c]
+                tree_copy(c, 0).wait_recv()
+                psum[:, cut] = (acc1[:, cut] + recv1[0, :, cut].astype(F32)).astype(BF16)
+                hand_out(c)
             else:
-                psum[:, cuts[c]] = term.astype(BF16)
-
-        def stage_b(c):
-            for b in range(low):
-                scatter_copy(c, b).wait_recv()
-                size = rows >> (b + 1)
-                term = acc1[seg(b + 1), cuts[c]] + recv1[b, 0:size, cuts[c]].astype(F32)
-                if b + 1 < low:
-                    acc1[seg(b + 1), cuts[c]] = term
-                    send1[seg(b + 1), cuts[c]] = term.astype(BF16)
-                    scatter_copy(c, b + 1).start()
-                else:
-                    psum[seg(low), cuts[c]] = term.astype(BF16)
-            across_copy(c).start()
-            spread(c)
+                reduce(c, 0)
 
         def part_copy(c, d):
             return remote(ubuf.at[i, :, ucuts[c]], ubuf.at[i, :, ucuts[c]], u_ss.at[0], u_rs.at[c], {"mp": lax.rem(i + d, n_mp)})
@@ -287,26 +284,28 @@
             def _():
                 for d in range(half):
                     pl.semaphore_signal(ready.at[0], inc=1, device_id={"mp": d}, device_id_type=MESH)
-                def pool_part(lag):
+                def pool_part(sends):
+                    lag = n1 if sends else 2
                     for c in range(n1 + lag):
                         if c < n1:
                             with scope(f"a{c}"):
-                                stage_a(c)
-                                if low > 0:
-                                    scatter_copy(c, 0).start()
+                                stage_a(c, sends)
                             if c == n1 - 1:
                                 w2_copy.start()
-                        if c >= lag:
+                        if c >= lag and not sends:
                             with scope(f"b{c - lag}"):
                                 stage_b(c - lag)
 
-                @pl.when(bit_of(0) == 0)
-                def _():
-                    pool_part(1)
-
-                @pl.when(bit_of(0) != 0)
-                def _():
-                    pool_part(2)
+                if low > 0:
+                    @pl.when(bit_of(0) == 0)
+                    def _():
+                        pool_part(True)
+
+                    @pl.when(bit_of(0) != 0)
+                    def _():
+                        pool_part(False)
+                else:
+                    pool_part(False)
 
             @pl.when(user_side)
             def _():
@@ -367,13 +366,14 @@
                             ucol_copy().start()
 
         def take_across(c):
-            @pl.when(user_side)
+            @pl.when(jnp.logical_and(user_side, root))
             def _():
                 with scope(f"across{c}"):
                     across_copy(c).wait_recv()
-                spread(c)
-
-        ahead = min(2, n1)
+                for b in range(low - 1, -1, -1):
+                    spread_copy(c, b).start()
+
+        ahead = 1
         with scope("bases"):
             w3_copy.start()
 
@@ -409,11 +409,17 @@
                     copy.wait()
 
         def first_cross(c):
-            with scope(f"gw{c}"):
-                for b in range(low - 1, -1, -1):
-                    gather_wait(c, b)
-                    if b > 0:
-                        gather_copy(c, b - 1).start()
+            if low > 0:
+                @pl.when(leaf)
+                def _():
+                    with scope(f"gw{c}"):
+                        spread_copy(c, 0).wait_recv()
+
+                for b in range(low - 2, -1, -1):
+                    @pl.when(jnp.logical_and(leaf, ones(b + 1)))
+                    def _():
+                        spread_copy(c, b).start()
+
             for u, ucut in enumerate(ucuts):
                 if ucut.start != cuts[c].start:
                     continue
@@ -462,14 +468,14 @@
 
         for c in range(n1):
             first_cross(c)
-            if c + ahead < n1:
-                take_across(c + ahead)
             if c == 0:
                 w2_copy.wait()
             if c < n1 - 1:
                 with scope(f"l2_{c}"):
                     term = jnp.dot(cross1[:, cuts[c]], w2_v[cuts[c], :], preferred_element_type=F32)
                     acc2[...] = term if c == 0 else acc2[...] + term
+            if c + ahead < n1:
+                take_across(c + ahead)
         even = bit_of(0) == 0
         odd = jnp.logical_not(even)
         detour = jnp.logical_and(even, j == n_cand - 1) if n_cand > 2 else None
@@ -594,12 +600,6 @@
                 )
                 acc3[r, cols] = term
                 send3[r, cols] = term.astype(BF16)
-            for peer in range(*spans[g]):
-                @pl.when(i != peer)
-                def _():
-                    for c in range(n3):
-                        last_copy(c, peer).start()
-
             count = r.stop - r.start
             lanes = jnp.zeros((count, 128), F32)
             for k in range(0, col, 128):
@@ -625,22 +625,31 @@
                 def _():
                     q_all[me] = q_mine[g]
 
+            for peer in range(*spans[g]):
+                @pl.when(i != peer)
+                def _():
+                    for c in range(n3):
+                        last_copy(c, peer).start()
+
         if q_width > 128:
             q_rows[...] = jnp.zeros(q_rows.shape, F32)
 
         def stream(skew, nears, passing, relays):
             ready_at = len(events) - skew if nears else 0
-            for s in range(len(events) + skew):
+            lag = min(5, len(events)) if relays else 0
+            for s in range(len(events) + skew + lag):
                 if nears and s < len(events):
                     near(*events[s])
-                    if relays == 1:
-                        relay(*events[s])
-                if s < skew:
+                back = s - lag if relays == 1 else s - skew - lag
+                if relays == 1 and 0 <= back < len(events):
+                    relay(*events[back])
+                if 0 <= s - skew < len(events):
+                    far(*events[s - skew], passing)
+                if relays == 2 and 0 <= back < len(events):
+                    relay(*events[back])
+                if not 0 <= s - skew < len(events):
                     continue
                 g, n = events[s - skew]
-                far(g, n, passing)
-                if relays == 2:
-                    relay(g, n)
                 if passing and not nears:
                     z_wait(g, n, nd)
                 with scope(f"third{g}_{n}"):
@@ -660,7 +669,7 @@
 
             @pl.when(jnp.logical_and(inner, jnp.logical_and(odd, left)))
             def _():
-                stream(min(11, len(events)), True, True, 2)
+                stream(min(13, len(events)), True, True, 2)
 
             @pl.when(jnp.logical_and(inner, jnp.logical_and(odd, jnp.logical_not(left))))
             def _():
@@ -668,7 +677,7 @@
 
             @pl.when(jnp.logical_and(inner, jnp.logical_and(even, left)))
             def _():
-                stream(min(11, len(events)), True, False, 0)
+                stream(len(events), True, False, 0)
 
             @pl.when(jnp.logical_and(inner, jnp.logical_and(even, jnp.logical_not(left))))
             def _():
@@ -699,11 +708,18 @@
             remote(ref, ref, sem, sem, {"cand": j}).wait_send()
 
         with scope("sent"):
-            @pl.when(pool_side)
-            def _():
-                for b in range(low):
-                    sent(recv1.at[b, pl.ds(0, rows >> (b + 1)), :], a_ss.at[b])
-                sent(psum.at[seg(low), :], x_ss.at[0])
+            for b in range(low):
+                @pl.when(jnp.logical_and(pool_side, jnp.logical_and(ones(b), bit_of(b) == 0)))
+                def _():
+                    sent(send1, a_ss.at[b])
+
+                @pl.when(ones(b + 1))
+                def _():
+                    sent(psum, g_ss.at[b])
+
+            @pl.when(jnp.logical_and(pool_side, root))
+            def _():
+                sent(psum, x_ss.at[0])
 
             @pl.when(user_side)
             def _():
@@ -719,8 +735,6 @@
 
                 sent(ubuf.at[pl.ds(0, n_mp - 1)], u_ss.at[0])
 
-            for b in range(low):
-                sent(psum.at[seg(b + 1), :], g_ss.at[b])
             @pl.when(end)
             def _():
                 sent(q_send, z_ss.at[nd])
@@ -761,8 +775,6 @@
         cuts = list(ucuts)
         half = n_mp // 2
         spans = [(0, half), (half, n_mp)]
-        if half > 1:
-            spans[1:] = [(half, half + half // 2), (half + half // 2, n_mp)]
         zcuts = []
         for lo, hi in spans:
             step = min(256 * half // (hi - lo), col, feat)
@@ -810,7 +822,7 @@
                 pltpu.VMEM((lhs_rows, feat), BF16),
                 pltpu.VMEM((rows, col), F32),
                 pltpu.VMEM((rows, col), BF16),
-                pltpu.VMEM((low, rows // 2, col), BF16),
+                pltpu.VMEM((low, rows, col), BF16),
                 pltpu.VMEM((rows, col), BF16),
                 pltpu.VMEM((n_mp, users, col), F32),
                 pltpu.VMEM((rows, col), BF16),
@@ -839,7 +851,7 @@
                 dma((1,)),
                 dma((n1,)),
                 dma((low,)),
-                dma((low, n1)),
+                dma((n1,)),
                 dma((1,)),
                 dma((len(ucuts),)),
                 dma((2,)),

time: 31.2 us -> 31.1 us (level)
  no operation moved by 1% of the time
where the time goes in v5:
time: 31.1 us; the launch traced here: 31 us
  Pallas kernels  29.5 us (95%)
  between operations  1.47 us (5%)
    pallas_call x1, Pallas kernels, body(): pl.pallas_call(make_kernel(n_mp, n_cand, shapes), out_shape=(pltpu.VMEM((...  28.8 us
    pallas_call x1, Pallas kernels, body(): pl.pallas_call(hand_on, out_shape=(jax.ShapeDtypeStruct((block, col), BF1...  0.65 us

profile of v5, /device:TPU:0, one launch (start us, length us, event | category | flops | bytes accessed | tf_op | source)
XLA Modules:
  0.0 31.0 jit_solution(10931796686643452947)
XLA Ops:
  1.3 28.8 %shard_map.122 = (bf16[16,2048]{1,0:T(8,128)(2,1)S(1)}, f32[1,16]{1,0:T(1,128)S(1)}) custom-call(bf16[1,4096]{1,0:T(2,128)(2,1)} %user_hbm.1, s32[1,1]{1,0:T(1,128)} %bitcast.5.slot_hbm, bf16[256,4096]{1,0:T(8,128)(2,1)} %pool_hbm.1, s32[1,64]{1,0:T(1,128)} %ids_hbm.1, bf16[2048,2048]{1,0:T(8,128)(2,1)} %w1_hbm.1, f32[1,2048]{1,0:T(1,128)} %bitcast.6, ...), custom_call_target="tpu_custom_call" | custom-call | tf_op jit(solution)/shard_map/pallas_call | solution.py:795
  30.1 0.7 %shard_map.123 = (bf16[16,2048]{1,0:T(8,128)(2,1)}, f32[1,16]{1,0:T(1,128)}) custom-call(bf16[16,2048]{1,0:T(8,128)(2,1)S(1)} %get-tuple-element.6.crossed_ref, f32[1,16]{1,0:T(1,128)S(1)} %get-tuple-element.7.logit_ref), custom_call_target="tpu_custom_call" | custom-call | tf_op jit(solution)/shard_map/pallas_call | solution.py:875

commit v6 on v5

--- a/solution.py
+++ b/solution.py
@@ -500,13 +500,18 @@
 
         def lend_copy(s):
             cols = slice(zcuts[0][s].start, zcuts[0][min(s + 1, len(zcuts[0]) - 1)].stop)
-            return remote(q_send.at[:, cols], qe.at[:, cols], qe_ss.at[0], qe_rs.at[s // 2], {"mp": i + 1 - 2 * bit_of(0)})
+            return remote(q_send.at[:, cols], qe.at[:, cols], qe_ss.at[0], qe_rs.at[0], {"mp": i + 1 - 2 * bit_of(0)})
 
         for s in range(0, len(zcuts[0]), 2):
             with scope(f"q{s}"):
-                for cols in zcuts[0][s : s + 2]:
-                    first_out(cols)
-                first_send(0, range(s, min(s + 2, len(zcuts[0]))))
+                if s == 0:
+                    for n in range(min(2, len(zcuts[0]))):
+                        first_out(zcuts[0][n])
+                        first_send(0, [n])
+                else:
+                    for cols in zcuts[0][s : s + 2]:
+                        first_out(cols)
+                    first_send(0, range(s, min(s + 2, len(zcuts[0]))))
 
                 @pl.when(jnp.logical_and(inner, even))
                 def _():
@@ -536,8 +541,8 @@
             k = place[g, n]
             with scope(f"relay{g}_{n}"):
                 remote(ze.at[at], ze.at[at], ef_ss.at[0], ze_rs.at[k], {"cand": j}).wait_recv()
-            if g == 0 and n % 2 == 0:
-                lend_copy(n).wait_recv()
+            if k == 0:
+                remote(q_send, qe, qe_ss.at[0], qe_rs.at[0], {"cand": j}).wait_recv()
             zf[at] = (ze[at].astype(F32) + qe[at].astype(F32)).astype(BF16)
 
             @pl.when(j > 1)
@@ -600,6 +605,14 @@
                 )
                 acc3[r, cols] = term
                 send3[r, cols] = term.astype(BF16)
+            def send_parts(lo, hi):
+                for peer in range(lo, hi):
+                    @pl.when(i != peer)
+                    def _():
+                        for c in range(n3):
+                            last_copy(c, peer).start()
+
+            send_parts(spans[g][0], spans[g][0] + 1)
             count = r.stop - r.start
             lanes = jnp.zeros((count, 128), F32)
             for k in range(0, col, 128):
@@ -625,11 +638,7 @@
                 def _():
                     q_all[me] = q_mine[g]
 
-            for peer in range(*spans[g]):
-                @pl.when(i != peer)
-                def _():
-                    for c in range(n3):
-                        last_copy(c, peer).start()
+            send_parts(spans[g][0] + 1, spans[g][1])
 
         if q_width > 128:
             q_rows[...] = jnp.zeros(q_rows.shape, F32)
@@ -782,7 +791,7 @@
         if step > 128:
             zcuts[-1][-1:] = [slice(feat - step, feat - step // 2), slice(feat - step // 2, feat)]
         n1 = len(cuts)
-        n3 = max(1, col // 512)
+        n3 = max(1, col // 1024)
         lhs_rows = -(-users // 16) * 16
         bits = n_mp.bit_length() - 1
         low = max(1, bits - 1)
@@ -858,7 +867,7 @@
                 dma((2, sum(len(part) for part in zcuts))),
                 dma((sum(len(part) for part in zcuts),)),
                 dma((1,)),
-                dma((-(-len(zcuts[0]) // 2),)),
+                dma((1,)),
                 dma((2,)),
                 dma((1,)),
                 dma((n3,)),

time: 31.1 us -> 31 us (level)
  no operation moved by 1% of the time
where the time goes in v6:
time: 31 us; the launch traced here: 30.8 us
  Pallas kernels  29.4 us (95%)
  between operations  1.47 us (5%)
    pallas_call x1, Pallas kernels, body(): pl.pallas_call(make_kernel(n_mp, n_cand, shapes), out_shape=(pltpu.VMEM((...  28.7 us
    pallas_call x1, Pallas kernels, body(): pl.pallas_call(hand_on, out_shape=(jax.ShapeDtypeStruct((block, col), BF1...  0.65 us

profile of v6, /device:TPU:0, one launch (start us, length us, event | category | flops | bytes accessed | tf_op | source)
XLA Modules:
  0.0 30.8 jit_solution(15658127942755580025)
XLA Ops:
  1.3 28.7 %shard_map.122 = (bf16[16,2048]{1,0:T(8,128)(2,1)S(1)}, f32[1,16]{1,0:T(1,128)S(1)}) custom-call(bf16[1,4096]{1,0:T(2,128)(2,1)} %user_hbm.1, s32[1,1]{1,0:T(1,128)} %bitcast.5.slot_hbm, bf16[256,4096]{1,0:T(8,128)(2,1)} %pool_hbm.1, s32[1,64]{1,0:T(1,128)} %ids_hbm.1, bf16[2048,2048]{1,0:T(8,128)(2,1)} %w1_hbm.1, f32[1,2048]{1,0:T(1,128)} %bitcast.6, ...), custom_call_target="tpu_custom_call" | custom-call | tf_op jit(solution)/shard_map/pallas_call | solution.py:804
  30.0 0.7 %shard_map.123 = (bf16[16,2048]{1,0:T(8,128)(2,1)}, f32[1,16]{1,0:T(1,128)}) custom-call(bf16[16,2048]{1,0:T(8,128)(2,1)S(1)} %get-tuple-element.6.crossed_ref, f32[1,16]{1,0:T(1,128)S(1)} %get-tuple-element.7.logit_ref), custom_call_target="tpu_custom_call" | custom-call | tf_op jit(solution)/shard_map/pallas_call | solution.py:884
